TPU v7x, 32 devices: a whole 2x2x4 slice. The times are simulated.
32 devices in a mesh: param: 16 (over z, x, core), qoi: 2 (over y).
Axes of the slice: x: 2, y: 2, z: 4, core: 2. Of those that a mesh axis runs over, the one named last changes fastest.
Arguments:
- samples: bfloat16 [16, 5120, 420], P('qoi', 'param'), may hold values from -6 to 6
- operator_rows: bfloat16 [8, 5120, 2, 512], P(None, 'param', None, 'qoi'), may hold values from -0.0625 to 0.0625
- block_start: int32 [1], replicated, may hold values from 0 to 203
- gauge_group: int32 [512], P('qoi'), may hold values from 0 to 15
Outputs:
- qoi_spectrum: float32 [16, 2, 8, 512], P('param', None, None, 'qoi')
- segment_response: float32 [16, 2, 8, 16], P('param')
Inputs may be any that keep to these rules, and one draw needn't show every extreme that they name: `block_start`: the block's frequencies lie among the 211 frequencies of a real transform.
All inputs are finite; a program needn't handle non-finite values.
Results may differ from a plain program's by a relative error of at most 0.005.
Values may be sent and summed in bfloat16 or wider, within the bound.
A program may use at most 64 MiB of HBM per device.

v0:
```python
import functools
import math

import jax
import jax.numpy as jnp
from jax import lax
from jax.experimental import pallas as pl
from jax.experimental.pallas import tpu as pltpu
from jax.sharding import PartitionSpec as P

GROUPS = 16
LANES = 128
CHUNKS = 1
PARTS = 2
MESH = pl.DeviceIdType.MESH
NT_DIMS = (((1,), (1,)), ((), ()))


def build_table(start, freq_count, steps_count, first, count, repeat):
    shape = (freq_count, count * repeat)
    steps = first + lax.broadcasted_iota(jnp.int32, shape, 1) // repeat
    freqs = lax.broadcasted_iota(jnp.int32, shape, 0) + start
    turns = (steps * freqs).astype(jnp.float32)
    whole = jnp.floor((turns + 0.5) * (1.0 / steps_count))
    phases = (turns - whole * steps_count) * (2.0 * math.pi / steps_count)
    table = jnp.concatenate([jnp.cos(phases), -jnp.sin(phases)], axis=0) * (
        1.0 / math.sqrt(steps_count)
    )
    high = table.astype(jnp.bfloat16).astype(jnp.float32)
    both = jnp.concatenate([high, table - high], axis=0)
    full = (4 * freq_count, repeat, count * repeat)
    keep = lax.broadcasted_iota(jnp.int32, full, 2) % repeat == lax.broadcasted_iota(
        jnp.int32, full, 1
    )
    wide = jnp.where(keep, both[:, None, :], 0.0)
    return wide.reshape(4 * freq_count * repeat, count * repeat).astype(jnp.bfloat16)


def kernel(
    param_count, qoi_count, start_hbm, group_hbm, samples_hbm, rows_hbm,
    out_ref, seg_ref,
    start_ref, group_ref, samples, weights, loose, dense, hot, line, product, outgoing, incoming, total, joined, shares, gathered,
    start_sem, group_sem, samples_sem, weights_sem, line_send, line_recv, out_send, out_recv, share_send, share_recv,
):
    steps_count, sample_local, param_local = samples.shape
    freq_count = weights.shape[0]
    gauge_local = group_ref.shape[1]
    halves = gauge_local // LANES
    sample_total = sample_local * qoi_count
    depth = 2 * param_local
    per_chunk = freq_count // CHUNKS
    me_p = lax.axis_index("param")
    me_q = lax.axis_index("qoi")

    barrier = pltpu.get_barrier_semaphore()
    for far in range(qoi_count):
        for offset in range(param_count):
            if far or offset:
                pl.semaphore_signal(
                    barrier,
                    inc=1,
                    device_id=(
                        lax.rem(me_p + offset, param_count), lax.rem(me_q + far, qoi_count)
                    ),
                    device_id_type=MESH,
                )

    start_copy = pltpu.make_async_copy(start_hbm, start_ref, start_sem)
    start_copy.start()
    group_copy = pltpu.make_async_copy(group_hbm, group_ref, group_sem)
    group_copy.start()
    edges = [steps_count * part // PARTS // 32 * 32 for part in range(PARTS)] + [steps_count]
    sample_copies = []
    for part in range(PARTS):
        picked = pl.ds(edges[part], edges[part + 1] - edges[part])
        copy = pltpu.make_async_copy(
            samples_hbm.at[picked], samples.at[picked], samples_sem.at[part]
        )
        copy.start()
        sample_copies.append(copy)
    start_copy.wait()
    start = start_ref[0]
    weight_copies = [
        pltpu.make_async_copy(rows_hbm.at[f], weights.at[f], weights_sem.at[f])
        for f in range(freq_count)
    ]
    both = None
    for part in range(PARTS):
        first, count = edges[part], edges[part + 1] - edges[part]
        table = build_table(start, freq_count, steps_count, first, count, sample_local)
        sample_copies[part].wait()
        if part == 0:
            for copy in weight_copies:
                copy.start()
        block = samples[pl.ds(first, count)].reshape(count * sample_local, param_local)
        term = jnp.dot(table, block, preferred_element_type=jnp.float32)
        both = term if both is None else both + term
    half = 2 * freq_count * sample_local
    spectrum = (both[:half] + both[half:]).astype(jnp.bfloat16)
    aligned = param_local // LANES * LANES
    parts = [spectrum[: half // 2], spectrum[half // 2 :]]
    pieces = [part[:, :aligned] for part in parts]
    if aligned < param_local:
        pieces.append(jnp.concatenate([part[:, aligned:] for part in parts], axis=1))
    line[me_q] = jnp.concatenate(pieces, axis=1).reshape(freq_count, sample_local, depth)

    pl.semaphore_wait(barrier, qoi_count * param_count - 1)
    line_copies = []
    for chunk in range(CHUNKS):
        picked = pl.ds(chunk * per_chunk, per_chunk)
        for offset in range(1, qoi_count):
            copy = pltpu.make_async_remote_copy(
                src_ref=line.at[me_q, picked],
                dst_ref=line.at[me_q, picked],
                send_sem=line_send.at[chunk, offset],
                recv_sem=line_recv.at[chunk, offset],
                device_id=(me_p, lax.rem(me_q + offset, qoi_count)),
                device_id_type=MESH,
            )
            copy.start()
            line_copies.append(copy)

    for f in range(freq_count):
        weight_copies[f].wait()
        loose[...] = weights[f].astype(jnp.float32)
        for j in range(halves):
            parts = [
                loose[pl.ds(2 * j + part, param_local, stride=2 * halves), :].astype(jnp.bfloat16)
                for part in range(2)
            ]
            dense[f, :, j * LANES : (j + 1) * LANES] = jnp.concatenate(
                [part[:aligned] for part in parts] + [part[aligned:] for part in parts], axis=0
            )

    group_copy.wait()
    columns = lax.broadcasted_iota(jnp.int32, (LANES, gauge_local), 0)
    for f in range(freq_count):
        hot[f] = (columns == group_ref[...] + f * GROUPS).astype(jnp.float32).astype(jnp.bfloat16)

    lane = lax.broadcasted_iota(jnp.int32, (1, depth), 1)
    tail = param_local - aligned
    second = ((lane >= aligned) & (lane < 2 * aligned)) | (lane >= 2 * aligned + tail)
    sign = jnp.where(second, -1.0, 1.0)
    out_copies = []
    order = list(range(1, param_count))
    stripe = 2 * per_chunk
    for chunk in range(CHUNKS):
        for offset in range(1, qoi_count):
            line_copies[chunk * (qoi_count - 1) + offset - 1].wait_recv()
        for f in range(chunk * per_chunk, (chunk + 1) * per_chunk):
            given = jnp.concatenate(
                [line[slot, f].astype(jnp.float32) for slot in range(qoi_count)], axis=0
            )
            real = given * sign
            swapped = [given[:, aligned : 2 * aligned], given[:, :aligned]]
            if tail:
                swapped.append(pltpu.roll(given[:, 2 * aligned :], tail, 1))
            left = jnp.concatenate([real, jnp.concatenate(swapped, axis=1)], axis=0)
            result = jnp.dot(
                left.astype(jnp.bfloat16), dense[f], preferred_element_type=jnp.float32
            )
            rows = 2 * sample_total
            sums = lax.dot_general(
                result.astype(jnp.bfloat16), hot[f], NT_DIMS, preferred_element_type=jnp.float32
            )
            segment = sums if f == 0 else segment + sums
            for j in range(halves):
                product[j, pl.ds(f * rows, rows), :] = result[:, j * LANES : (j + 1) * LANES]
        for r in range(sample_total):
            for j in range(halves):
                outgoing[r, chunk, :, j * LANES : (j + 1) * LANES] = product[
                    j,
                    pl.ds(chunk * per_chunk * 2 * sample_total + r, stripe, stride=sample_total),
                    :,
                ].astype(jnp.bfloat16)
        if chunk == CHUNKS - 1:
            joined[...] = segment * math.sqrt(GROUPS / (gauge_local * qoi_count))
            for k in range(sample_total):
                shares[k] = joined[pl.ds(k, 2, stride=sample_total), :]
            mine = me_q * param_count + me_p
            gathered[mine] = shares[me_p]
            seg_copies = []
            for far in reversed(range(qoi_count)):
                for offset in order + [0]:
                    if far == 0 and offset == 0:
                        continue
                    target = lax.rem(me_p + offset, param_count)
                    copy = pltpu.make_async_remote_copy(
                        src_ref=shares.at[target],
                        dst_ref=gathered.at[mine],
                        send_sem=share_send.at[far * param_count + offset],
                        recv_sem=share_recv.at[far * param_count + offset],
                        device_id=(target, lax.rem(me_q + far, qoi_count)),
                        device_id_type=MESH,
                    )
                    copy.start()
                    seg_copies.append(copy)
        for offset in order:
            target = lax.rem(me_p + offset, param_count)
            copy = pltpu.make_async_remote_copy(
                src_ref=outgoing.at[target, chunk],
                dst_ref=incoming.at[offset, chunk],
                send_sem=out_send.at[chunk, offset],
                recv_sem=out_recv.at[chunk, offset],
                device_id=(target, me_q),
                device_id_type=MESH,
            )
            copy.start()
            out_copies.append(copy)

    for chunk in range(CHUNKS):
        partial = outgoing[me_p, chunk].astype(jnp.float32)
        for index, offset in reversed(list(enumerate(order))):
            out_copies[chunk * (param_count - 1) + index].wait_recv()
            partial = partial + incoming[offset, chunk].astype(jnp.float32)
        for j in range(halves):
            total[j, pl.ds(chunk * stripe, stripe), :] = partial[:, j * LANES : (j + 1) * LANES]
    ordered = jnp.concatenate(
        [
            jnp.concatenate(
                [total[j, pl.ds(part, freq_count, stride=2), :] for j in range(halves)], axis=1
            )
            for part in range(2)
        ],
        axis=0,
    )
    out_ref[...] = ordered.reshape(out_ref.shape)
    for copy in line_copies + out_copies:
        copy.wait_send()
    for copy in seg_copies:
        copy.wait()
    final = gathered[0]
    for p in range(1, param_count * qoi_count):
        final = final + gathered[p]
    seg_ref[...] = final.reshape(seg_ref.shape)


def local(samples, operator_rows, block_start, gauge_group):
    sample_local, param_local, steps_count = samples.shape
    freq_count, _, _, gauge_local = operator_rows.shape
    param_count, qoi_count = lax.axis_size("param"), lax.axis_size("qoi")
    sample_total = sample_local * qoi_count
    halves = gauge_local // LANES
    depth = 2 * param_local
    stripe = 2 * freq_count // CHUNKS
    assert sample_total == param_count and freq_count * GROUPS == LANES
    rows = operator_rows.reshape(freq_count, param_local, 2, halves, LANES)
    rows = rows.transpose(0, 1, 3, 2, 4).reshape(freq_count, depth * halves, LANES)
    dma = pltpu.SemaphoreType.DMA
    vmem = pl.BlockSpec(memory_space=pltpu.VMEM)
    hbm = pl.BlockSpec(memory_space=pltpu.HBM)
    qoi_spectrum, response = pl.pallas_call(
        functools.partial(kernel, param_count, qoi_count),
        out_shape=(
            jax.ShapeDtypeStruct((1, 2, freq_count, gauge_local), jnp.float32),
            jax.ShapeDtypeStruct((1, 2, freq_count * GROUPS), jnp.float32),
        ),
        in_specs=[
            pl.BlockSpec(memory_space=pl.ANY),
            hbm,
            hbm,
            hbm,
        ],
        out_specs=(vmem, vmem),
        scratch_shapes=[
            pltpu.SMEM((1,), jnp.int32),
            pltpu.VMEM((1, gauge_local), jnp.int32),
            pltpu.VMEM((steps_count, sample_local, param_local), jnp.bfloat16),
            pltpu.VMEM((freq_count, depth * halves, LANES), jnp.bfloat16),
            pltpu.VMEM((depth * halves, LANES), jnp.float32),
            pltpu.VMEM((freq_count, depth, gauge_local), jnp.bfloat16),
            pltpu.VMEM((freq_count, LANES, gauge_local), jnp.bfloat16),
            pltpu.VMEM((qoi_count, freq_count, sample_local, depth), jnp.bfloat16),
            pltpu.VMEM((halves, freq_count * 2 * sample_total, LANES), jnp.float32),
            pltpu.VMEM((sample_total, CHUNKS, stripe, gauge_local), jnp.bfloat16),
            pltpu.VMEM((param_count, CHUNKS, stripe, gauge_local), jnp.bfloat16),
            pltpu.VMEM((halves, 2 * freq_count, LANES), jnp.float32),
            pltpu.VMEM((2 * sample_total, LANES), jnp.float32),
            pltpu.VMEM((sample_total, 2, LANES), jnp.float32),
            pltpu.VMEM((qoi_count * param_count, 2, LANES), jnp.float32),
            dma(()),
            dma(()),
            dma((PARTS,)),
            dma((freq_count,)),
            dma((CHUNKS, qoi_count)),
            dma((CHUNKS, qoi_count)),
            dma((CHUNKS, param_count)),
            dma((CHUNKS, param_count)),
            dma((qoi_count * param_count,)),
            dma((qoi_count * param_count,)),
        ],
        compiler_params=pltpu.CompilerParams(collective_id=0, has_side_effects=True, vmem_limit_bytes=53 * 2**20),
    )(block_start, gauge_group.reshape(1, gauge_local), samples.transpose(2, 0, 1), rows)
    return qoi_spectrum, response.reshape(1, 2, freq_count, GROUPS)


def solution(mesh):
    return jax.shard_map(
        local,
        mesh=mesh,
        in_specs=(P("qoi", "param", None), P(None, "param", None, "qoi"), P(), P("qoi")),
        out_specs=(P("param", None, None, "qoi"), P("param", None, None, None)),
        check_vma=False,
    )
```

profile of v0, /device:TPU:0, one launch (start us, length us, event | category | flops | bytes accessed | tf_op | source)
XLA Modules:
  0.0 20.3 jit_solution(11532010931568962464)
XLA Ops:
  1.3 0.0 copy-start
  1.3 0.7 %copy-done = s32[256]{0:T(256)S(1)} copy-done((s32[256]{0:T(256)S(1)}, s32[256]{0:T(256)}, u32[]{:S(2)}) %copy-start) | copy-done | bytes 1048
  2.0 17.0 %shard_map.59 = (f32[1,2,8,256]{3,2,1,0:T(8,128)S(1)}, f32[1,2,128]{2,1,0:T(2,128)S(1)}) custom-call(s32[1]{0:T(128)S(6)} %copy.8.start_hbm, s32[1,256]{1,0:T(1,128)S(1)} %bitcast.7, bf16[420,8,320]{2,1,0:T(8,128)(2,1)} %bitcast.9, bf16[8,1280,128]{2,1,0:T(8,128)(2,1)} %bitcast.8), custom_call_target="tpu_custom_call" | custom-call | tf_op jit(solution)/shard_map/pallas_call | solution.py:252
  19.0 0.7 %reshape.19 = f32[1,2,8,16]{3,2,1,0:T(8,128)} reshape(f32[1,2,128]{2,1,0:T(2,128)S(1)} %get-tuple-element.5) | data formatting | bytes 2048 | tf_op jit(solution)/shard_map/reshape | solution.py:294
  19.7 0.6 %copy.9 = f32[1,2,8,256]{3,2,1,0:T(8,128)} copy(f32[1,2,8,256]{3,2,1,0:T(8,128)S(1)} %get-tuple-element.8) | data formatting | bytes 32768
Async XLA Ops:
  1.3 0.7 %copy-start = (s32[256]{0:T(256)S(1)}, s32[256]{0:T(256)}, u32[]{:S(2)}) copy-start(s32[256]{0:T(256)} %param.7) | copy-start | bytes 3076
where the time goes:
time: 20.5 us; the launch traced here: 20.3 us
  Pallas kernels  17 us (83%)
  local copies, waits for them, and re-layouts  1.96 us (10%)
  between operations  1.29 us (6%)
    pallas_call x1, Pallas kernels, local(): pl.pallas_call(functools.partial(kernel, param_count, qoi_count), out_sha...  17 us
    unnamed x3, local copies, waits for them, and re-layouts  1.28 us
    reshape x1, local copies, waits for them, and re-layouts, local(): return (qoi_spectrum, response.reshape(1, 2, freq_count, GROUPS))  0.68 us

commit v1 on v0

v1 whole, which is shorter than its diff:
```python
import functools
import math

import jax
import jax.numpy as jnp
from jax import lax
from jax.experimental import pallas as pl
from jax.experimental.pallas import tpu as pltpu
from jax.sharding import PartitionSpec as P

GROUPS = 16
LANES = 128
PARTS = 4
LOADS = 4
MESH = pl.DeviceIdType.MESH
NT_DIMS = (((1,), (1,)), ((), ()))


def build_table(start, freq_count, steps_count, repeat, table):
    shape = (freq_count, steps_count * repeat)
    steps = lax.broadcasted_iota(jnp.int32, shape, 1) // repeat
    freqs = lax.broadcasted_iota(jnp.int32, shape, 0) + start
    turns = (steps * freqs).astype(jnp.float32)
    whole = jnp.floor((turns + 0.5) * (1.0 / steps_count))
    phases = (turns - whole * steps_count) * (2.0 * math.pi / steps_count)
    scale = 1.0 / math.sqrt(steps_count)
    waves = [jnp.cos(phases) * scale, jnp.sin(phases) * -scale]
    highs = [wave.astype(jnp.bfloat16).astype(jnp.float32) for wave in waves]
    lows = [wave - high for wave, high in zip(waves, highs)]
    full = (repeat, steps_count * repeat)
    keep = lax.broadcasted_iota(jnp.int32, full, 1) % repeat == lax.broadcasted_iota(
        jnp.int32, full, 0
    )
    for level, pair in enumerate((highs, lows)):
        for f in range(freq_count):
            rows = jnp.concatenate(
                [jnp.where(keep, jnp.broadcast_to(wave[f : f + 1], full), 0.0) for wave in pair],
                axis=0,
            )
            first = (level * freq_count + f) * 2 * repeat
            table[pl.ds(first, 2 * repeat), :] = rows.astype(jnp.bfloat16)


def kernel(
    param_count, qoi_count, start_ref, group_hbm, samples_hbm, rows_hbm,
    out_ref, seg_ref,
    group_ref, samples, table, weights, loose, dense, dense_tail, hot, line, line_tail, product, outgoing, incoming, joined, shares, gathered,
    group_sem, samples_sem, weights_sem, line_send, line_recv, out_send, out_recv, share_send, share_recv,
):
    steps_count, sample_local, param_local = samples.shape
    freq_count = weights.shape[0]
    gauge_local = group_ref.shape[1]
    halves = gauge_local // LANES
    sample_total = sample_local * qoi_count
    aligned = param_local // LANES * LANES
    tail = param_local - aligned
    pair_rows = 2 * sample_local
    half_freqs = freq_count // 2
    me_p = lax.axis_index("param")
    me_q = lax.axis_index("qoi")

    edges = [steps_count * part // PARTS // 32 * 32 for part in range(PARTS)] + [steps_count]
    spans = [pl.ds(edges[part], edges[part + 1] - edges[part]) for part in range(PARTS)]
    sample_copies = [
        pltpu.make_async_copy(samples_hbm.at[span], samples.at[span], samples_sem.at[part])
        for part, span in enumerate(spans)
    ]
    for copy in sample_copies:
        copy.start()
    group_copy = pltpu.make_async_copy(group_hbm, group_ref, group_sem)
    group_copy.start()
    per_load = freq_count // LOADS
    loads = [pl.ds(load * per_load, per_load) for load in range(LOADS)]
    weight_copies = [
        pltpu.make_async_copy(rows_hbm.at[load], weights.at[load], weights_sem.at[index])
        for index, load in enumerate(loads)
    ]

    barrier = pltpu.get_barrier_semaphore()
    for far in range(qoi_count):
        for offset in range(param_count):
            if far or offset:
                pl.semaphore_signal(
                    barrier,
                    inc=1,
                    device_id=(
                        lax.rem(me_p + offset, param_count), lax.rem(me_q + far, qoi_count)
                    ),
                    device_id_type=MESH,
                )

    build_table(start_ref[0], freq_count, steps_count, sample_local, table)

    main = ends = None
    for part in range(PARTS):
        first, count = edges[part], edges[part + 1] - edges[part]
        sample_copies[part].wait()
        if part == PARTS // 2:
            for copy in weight_copies:
                copy.start()
        block = samples[spans[part]].reshape(count * sample_local, param_local)
        turn = table[:, first * sample_local : (first + count) * sample_local]
        term = jnp.dot(turn, block[:, :aligned], preferred_element_type=jnp.float32)
        last = jnp.dot(turn, block[:, aligned:], preferred_element_type=jnp.float32)
        main = term if main is None else main + term
        ends = last if ends is None else ends + last
    half = 2 * freq_count * sample_local
    spectrum = (main[:half] + main[half:]).astype(jnp.bfloat16)
    for chunk in range(aligned // LANES):
        line[chunk, me_q] = spectrum[:, chunk * LANES : (chunk + 1) * LANES].reshape(
            freq_count, pair_rows, LANES
        )
    spectrum = ends[:half] + ends[half:]
    line_tail[me_q] = (
        jnp.concatenate([spectrum[: half // 2], spectrum[half // 2 :]], axis=1)
        .astype(jnp.bfloat16)
        .reshape(half_freqs, pair_rows, 2 * tail)
    )

    pl.semaphore_wait(barrier, qoi_count * param_count - 1)
    buffers = [line.at[chunk] for chunk in range(aligned // LANES)] + [line_tail]
    line_waits = []
    for index, buffer in enumerate(buffers):
        for offset in range(1, qoi_count):
            pltpu.make_async_remote_copy(
                src_ref=buffer.at[me_q],
                dst_ref=buffer.at[me_q],
                send_sem=line_send.at[index],
                recv_sem=line_recv.at[index],
                device_id=(me_p, lax.rem(me_q + offset, qoi_count)),
                device_id_type=MESH,
            ).start()
        others = buffer.at[pl.ds(0, qoi_count - 1)]
        line_waits.append(
            pltpu.make_async_remote_copy(
                src_ref=others,
                dst_ref=others,
                send_sem=line_send.at[index],
                recv_sem=line_recv.at[index],
                device_id=(me_p, lax.rem(me_q + 1, qoi_count)),
                device_id_type=MESH,
            )
        )

    for f in range(freq_count):
        if f % per_load == 0:
            weight_copies[f // per_load].wait()
        loose[...] = weights[f].astype(jnp.float32)
        for j in range(halves):
            columns = pl.ds(j * LANES, LANES)
            for part in range(2):
                piece = loose[
                    pl.ds(2 * j + part, param_local, stride=2 * halves), :
                ].astype(jnp.bfloat16)
                dense[f, part, :, columns] = piece[:aligned]
                dense_tail[f % half_freqs, part, pl.ds(f // half_freqs * tail, tail), columns] = (
                    piece[aligned:]
                )

    group_copy.wait()
    slots = lax.broadcasted_iota(jnp.int32, (LANES, gauge_local), 0)
    for f in range(freq_count):
        place = (freq_count - f) % freq_count * GROUPS
        hot[f] = (slots == group_ref[...] + place).astype(jnp.float32).astype(jnp.bfloat16)

    def combine(real_side, imag_side):
        reals, imags = [], []
        for q in range(qoi_count):
            low, mid, high = q * pair_rows, q * pair_rows + sample_local, (q + 1) * pair_rows
            reals.append(real_side[low:mid] - imag_side[mid:high])
            imags.append(imag_side[low:mid] + real_side[mid:high])
        return [jnp.concatenate(reals, axis=0), jnp.concatenate(imags, axis=0)]

    def place_of(k, f):
        return pl.ds((k * freq_count + f) * sample_total, sample_total)

    for chunk in range(aligned // LANES):
        line_waits[chunk].wait_recv()
        for f in range(freq_count):
            left = jnp.concatenate([line[chunk, q, f] for q in range(qoi_count)], axis=0)
            sides = [
                jnp.dot(
                    left,
                    dense[f, part, chunk * LANES : (chunk + 1) * LANES, :],
                    preferred_element_type=jnp.float32,
                )
                for part in range(2)
            ]
            for k, value in enumerate(combine(*sides)):
                for j in range(halves):
                    here = value[:, j * LANES : (j + 1) * LANES]
                    if chunk:
                        here = here + product[j, place_of(k, f), :]
                    product[j, place_of(k, f), :] = here

    line_waits[-1].wait_recv()
    lane = lax.broadcasted_iota(jnp.int32, (qoi_count * pair_rows, 2 * tail), 1)
    segment = None
    for f in range(freq_count):
        left = jnp.concatenate(
            [line_tail[q, f % half_freqs] for q in range(qoi_count)], axis=0
        )
        left = jnp.where((lane >= tail) == (f >= half_freqs), left.astype(jnp.float32), 0.0)
        left = left.astype(jnp.bfloat16)
        sides = [
            jnp.dot(left, dense_tail[f % half_freqs, part], preferred_element_type=jnp.float32)
            for part in range(2)
        ]
        finals = []
        for k, value in enumerate(combine(*sides)):
            wide = []
            for j in range(halves):
                here = value[:, j * LANES : (j + 1) * LANES] + product[j, place_of(k, f), :]
                product[j, place_of(k, f), :] = here
                wide.append(here)
            finals.append(jnp.concatenate(wide, axis=1))
        sums = lax.dot_general(
            jnp.concatenate(finals, axis=0).astype(jnp.bfloat16),
            hot[f],
            NT_DIMS,
            preferred_element_type=jnp.float32,
        )
        segment = sums if segment is None else segment + sums
    stripe = 2 * freq_count
    for r in range(sample_total):
        for j in range(halves):
            outgoing[r, :, j * LANES : (j + 1) * LANES] = product[
                j, pl.ds(r, stripe, stride=sample_total), :
            ].astype(jnp.bfloat16)
    for offset in range(1, param_count):
        target = lax.rem(me_p + offset, param_count)
        pltpu.make_async_remote_copy(
            src_ref=outgoing.at[target],
            dst_ref=incoming.at[me_p],
            send_sem=out_send,
            recv_sem=out_recv,
            device_id=(target, me_q),
            device_id_type=MESH,
        ).start()
    joined[...] = segment * math.sqrt(GROUPS / (gauge_local * qoi_count))
    for k in range(sample_total):
        shares[k] = joined[pl.ds(k, 2, stride=sample_total), :]
    mine = me_q * param_count + me_p
    for far in reversed(range(qoi_count)):
        for offset in range(param_count):
            if far or offset:
                target = lax.rem(me_p + offset, param_count)
                pltpu.make_async_remote_copy(
                    src_ref=shares.at[target],
                    dst_ref=gathered.at[mine],
                    send_sem=share_send,
                    recv_sem=share_recv,
                    device_id=(target, lax.rem(me_q + far, qoi_count)),
                    device_id_type=MESH,
                ).start()
    incoming[me_p] = outgoing[me_p]
    gathered[mine] = shares[me_p]

    aside = (lax.rem(me_p + 1, param_count), me_q)
    others = incoming.at[pl.ds(0, param_count - 1)]
    out_wait = pltpu.make_async_remote_copy(
        src_ref=others, dst_ref=others, send_sem=out_send, recv_sem=out_recv,
        device_id=aside, device_id_type=MESH,
    )
    others = gathered.at[pl.ds(0, qoi_count * param_count - 1)]
    share_wait = pltpu.make_async_remote_copy(
        src_ref=others, dst_ref=others, send_sem=share_send, recv_sem=share_recv,
        device_id=aside, device_id_type=MESH,
    )
    out_wait.wait_recv()
    total = incoming[0].astype(jnp.float32)
    for p in range(1, param_count):
        total = total + incoming[p].astype(jnp.float32)
    out_ref[...] = total.reshape(out_ref.shape)
    share_wait.wait_recv()
    final = gathered[0]
    for p in range(1, param_count * qoi_count):
        final = final + gathered[p]
    for k in range(2):
        rows = jnp.broadcast_to(final[k : k + 1], (freq_count, LANES))
        turned = pltpu.roll(rows, 0, 1, stride=GROUPS, stride_axis=0)
        seg_ref[0, k] = turned[:, :GROUPS]
    for wait in line_waits:
        wait.wait_send()
    out_wait.wait_send()
    share_wait.wait_send()


def writer(spectrum_ref, response_ref, spectrum_hbm, response_hbm, sems):
    copies = [
        pltpu.make_async_copy(spectrum_ref, spectrum_hbm, sems.at[0]),
        pltpu.make_async_copy(response_ref, response_hbm, sems.at[1]),
    ]
    for copy in copies:
        copy.start()
    for copy in copies:
        copy.wait()


def local(samples, operator_rows, block_start, gauge_group):
    sample_local, param_local, steps_count = samples.shape
    freq_count, _, _, gauge_local = operator_rows.shape
    param_count, qoi_count = lax.axis_size("param"), lax.axis_size("qoi")
    sample_total = sample_local * qoi_count
    halves = gauge_local // LANES
    depth = 2 * param_local
    stripe = 2 * freq_count
    aligned = param_local // LANES * LANES
    tail = param_local - aligned
    assert sample_total == param_count and freq_count * GROUPS == LANES
    assert 2 * tail == LANES and freq_count % LOADS == 0
    rows = operator_rows.reshape(freq_count, param_local, 2, halves, LANES)
    rows = rows.transpose(0, 1, 3, 2, 4).reshape(freq_count, depth * halves, LANES)
    dma = pltpu.SemaphoreType.DMA
    vmem = pl.BlockSpec(memory_space=pltpu.VMEM)
    hbm = pl.BlockSpec(memory_space=pltpu.HBM)
    shapes = (
        jax.ShapeDtypeStruct((1, 2, freq_count, gauge_local), jnp.float32),
        jax.ShapeDtypeStruct((1, 2, freq_count, GROUPS), jnp.float32),
    )
    found = pl.pallas_call(
        functools.partial(kernel, param_count, qoi_count),
        out_shape=shapes,
        in_specs=[pl.BlockSpec(memory_space=pltpu.SMEM), hbm, hbm, hbm],
        out_specs=(vmem, vmem),
        scratch_shapes=[
            pltpu.VMEM((1, gauge_local), jnp.int32),
            pltpu.VMEM((steps_count, sample_local, param_local), jnp.bfloat16),
            pltpu.VMEM((4 * freq_count * sample_local, steps_count * sample_local), jnp.bfloat16),
            pltpu.VMEM((freq_count, depth * halves, LANES), jnp.bfloat16),
            pltpu.VMEM((depth * halves, LANES), jnp.float32),
            pltpu.VMEM((freq_count, 2, aligned, gauge_local), jnp.bfloat16),
            pltpu.VMEM((freq_count // 2, 2, 2 * tail, gauge_local), jnp.bfloat16),
            pltpu.VMEM((freq_count, LANES, gauge_local), jnp.bfloat16),
            pltpu.VMEM((aligned // LANES, qoi_count, freq_count, 2 * sample_local, LANES), jnp.bfloat16),
            pltpu.VMEM((qoi_count, freq_count // 2, 2 * sample_local, 2 * tail), jnp.bfloat16),
            pltpu.VMEM((halves, stripe * sample_total, LANES), jnp.float32),
            pltpu.VMEM((sample_total, stripe, gauge_local), jnp.bfloat16),
            pltpu.VMEM((param_count, stripe, gauge_local), jnp.bfloat16),
            pltpu.VMEM((2 * sample_total, LANES), jnp.float32),
            pltpu.VMEM((sample_total, 2, LANES), jnp.float32),
            pltpu.VMEM((qoi_count * param_count, 2, LANES), jnp.float32),
            dma(()),
            dma((PARTS,)),
            dma((LOADS,)),
            dma((aligned // LANES + 1,)),
            dma((aligned // LANES + 1,)),
            dma(()),
            dma(()),
            dma(()),
            dma(()),
        ],
        compiler_params=pltpu.CompilerParams(
            collective_id=0, has_side_effects=True, vmem_limit_bytes=53 * 2**20
        ),
    )(
        block_start,
        pltpu.with_memory_space_constraint(gauge_group.reshape(1, gauge_local), pltpu.HBM),
        samples.transpose(2, 0, 1),
        rows,
    )
    return pl.pallas_call(
        writer,
        out_shape=shapes,
        in_specs=[vmem, vmem],
        out_specs=(pl.BlockSpec(memory_space=pl.ANY), pl.BlockSpec(memory_space=pl.ANY)),
        scratch_shapes=[dma((2,))],
    )(*[pltpu.with_memory_space_constraint(array, pltpu.VMEM) for array in found])


def solution(mesh):
    return jax.shard_map(
        local,
        mesh=mesh,
        in_specs=(P("qoi", "param", None), P(None, "param", None, "qoi"), P(), P("qoi")),
        out_specs=(P("param", None, None, "qoi"), P("param", None, None, None)),
        check_vma=False,
    )
```

time: 20.5 us -> 18.6 us (0.907)
  local copies, waits for them, and re-layouts: 1.96 us -> 0 us
    unnamed x3 -> x0, local copies, waits for them, and re-layouts: 1.28 us -> none
    reshape x1 -> x0, local copies, waits for them, and re-layouts: 0.68 us -> none  [local(): return (qoi_spectrum, response.reshape(1, 2, freq_count, GROUPS))]
    pallas_call x0 -> x1, Pallas kernels: none -> 0.63 us  [local(): pl.pallas_call(writer, out_shape=shapes, in_specs=[vmem, vmem], out_specs...]
    pallas_call x1, Pallas kernels: 17 us -> 16.5 us  [local(): pl.pallas_call(functools.partial(kernel, param_count, qoi_count), out_sha...]
where the time goes in v1:
time: 18.6 us; the launch traced here: 18.4 us
  Pallas kernels  17.1 us (92%)
  between operations  1.28 us (7%)
    pallas_call x1, Pallas kernels, local(): pl.pallas_call(functools.partial(kernel, param_count, qoi_count), out_sha...  16.5 us
    pallas_call x1, Pallas kernels, local(): pl.pallas_call(writer, out_shape=shapes, in_specs=[vmem, vmem], out_specs...  0.63 us

profile of v1, /device:TPU:0, one launch (start us, length us, event | category | flops | bytes accessed | tf_op | source)
XLA Modules:
  0.0 18.4 jit_solution(11606190627050624296)
XLA Ops:
  1.3 16.5 %shard_map.59 = (f32[1,2,8,256]{3,2,1,0:T(8,128)S(1)}, f32[1,2,8,16]{3,2,1,0:T(8,128)S(1)}) custom-call(s32[1]{0:T(128)S(6)} %copy.7.start_ref, s32[1,256]{1,0:T(1,128)} %bitcast.9, bf16[420,8,320]{2,1,0:T(8,128)(2,1)} %bitcast.8, bf16[8,1280,128]{2,1,0:T(8,128)(2,1)} %bitcast.7), custom_call_target="tpu_custom_call" | custom-call | tf_op jit(solution)/shard_map/pallas_call | solution.py:321
  17.8 0.6 %shard_map.60 = (f32[1,2,8,256]{3,2,1,0:T(8,128)}, f32[1,2,8,16]{3,2,1,0:T(8,128)}) custom-call(f32[1,2,8,256]{3,2,1,0:T(8,128)S(1)} %get-tuple-element.4.spectrum_ref, f32[1,2,8,16]{3,2,1,0:T(8,128)S(1)} %get-tuple-element.5.response_ref), custom_call_target="tpu_custom_call" | custom-call | tf_op jit(solution)/shard_map/pallas_call | solution.py:362

commit v2 on v1

v2 whole, which is shorter than its diff:
```python
import functools
import math

import jax
import jax.numpy as jnp
from jax import lax
from jax.experimental import pallas as pl
from jax.experimental.pallas import tpu as pltpu
from jax.sharding import PartitionSpec as P

GROUPS = 16
LANES = 128
LOADS = 4
MESH = pl.DeviceIdType.MESH
NT_DIMS = (((1,), (1,)), ((), ()))


def build_table(start, freq_count, steps_count, count, repeat, table):
    shape = (freq_count, count * repeat)
    steps = lax.broadcasted_iota(jnp.int32, shape, 1) // repeat
    freqs = lax.broadcasted_iota(jnp.int32, shape, 0) + start
    turns = (steps * freqs).astype(jnp.float32)
    whole = jnp.floor((turns + 0.5) * (1.0 / steps_count))
    phases = (turns - whole * steps_count) * (2.0 * math.pi / steps_count)
    scale = 1.0 / math.sqrt(steps_count)
    waves = [jnp.cos(phases) * scale, jnp.sin(phases) * -scale]
    highs = [wave.astype(jnp.bfloat16).astype(jnp.float32) for wave in waves]
    lows = [wave - high for wave, high in zip(waves, highs)]
    full = (repeat, count * repeat)
    keep = lax.broadcasted_iota(jnp.int32, full, 1) % repeat == lax.broadcasted_iota(
        jnp.int32, full, 0
    )
    for level, pair in enumerate((highs, lows)):
        for f in range(freq_count):
            rows = jnp.concatenate(
                [jnp.where(keep, jnp.broadcast_to(wave[f : f + 1], full), 0.0) for wave in pair],
                axis=0,
            )
            first = (level * freq_count + f) * 2 * repeat
            table[pl.ds(first, 2 * repeat), :] = rows.astype(jnp.bfloat16)


def kernel(
    param_count, qoi_count, start_ref, group_hbm, samples_hbm, rows_hbm,
    out_ref, seg_ref,
    group_ref, samples, table, weights, loose, dense, dense_tail, hot, line, line_tail, near, far, outgoing, incoming, joined, shares, gathered,
    group_sem, samples_sem, weights_sem, line_send, line_recv, out_send, out_recv, share_send, share_recv, known,
):
    steps_count, sample_local, param_local = samples.shape
    freq_count = weights.shape[0]
    gauge_local = group_ref.shape[1]
    halves = gauge_local // LANES
    aligned = param_local // LANES * LANES
    tail = param_local - aligned
    chunks = aligned // LANES
    pair_rows = 2 * sample_local
    half_freqs = freq_count // 2
    half_steps = steps_count // 2
    stripe = 2 * freq_count
    inner = 2 ** (int(math.log2(param_count)) // 2)
    me_p = lax.axis_index("param")
    me_q = lax.axis_index("qoi")
    base = me_p // inner * inner

    contacts = []
    for turn in range(1, param_count // inner):
        contacts.append((lax.rem(me_p + turn * inner, param_count), me_q))
    for other in reversed(range(qoi_count)):
        for turn in range(inner):
            if other or turn:
                contacts.append(
                    (base + lax.rem(me_p + turn, inner), lax.rem(me_q + other, qoi_count))
                )
    barrier = pltpu.get_barrier_semaphore()
    spans = [pl.ds(0, half_steps), pl.ds(half_steps, half_steps)]
    sample_copies = [
        pltpu.make_async_copy(samples_hbm.at[span], samples.at[span], samples_sem.at[part])
        for part, span in enumerate(spans)
    ]
    for copy in sample_copies:
        copy.start()
    for contact in contacts:
        pl.semaphore_signal(barrier, inc=1, device_id=contact, device_id_type=MESH)
    group_copy = pltpu.make_async_copy(group_hbm, group_ref, group_sem)
    group_copy.start()
    per_load = freq_count // LOADS
    loads = [pl.ds(load * per_load, per_load) for load in range(LOADS)]
    weight_copies = [
        pltpu.make_async_copy(rows_hbm.at[load], weights.at[load], weights_sem.at[index])
        for index, load in enumerate(loads)
    ]

    start = start_ref[0]
    build_table(start, freq_count, steps_count, half_steps, sample_local, table)

    turns = table[...]
    blocks, sides = [], []
    half = freq_count * pair_rows
    for part in range(2):
        sample_copies[part].wait()
        if part == 0:
            for copy in weight_copies:
                copy.start()
        block = samples[spans[part]].reshape(half_steps * sample_local, param_local)
        both = jnp.dot(turns, block[:, :aligned], preferred_element_type=jnp.float32)
        sides.append(both[:half] + both[half:])
        blocks.append(block[:, aligned:])
    odd = lax.rem(start + lax.broadcasted_iota(jnp.int32, (half, LANES), 0) // pair_rows, 2)
    sign = 1.0 - 2.0 * odd.astype(jnp.float32)
    for chunk in range(chunks):
        columns = slice(chunk * LANES, (chunk + 1) * LANES)
        spectrum = sides[0][:, columns] + sign * sides[1][:, columns]
        line[chunk, me_q] = spectrum.astype(jnp.bfloat16).reshape(freq_count, pair_rows, LANES)
    both = jnp.dot(turns, jnp.concatenate(blocks, axis=1), preferred_element_type=jnp.float32)
    both = both[:half] + both[half:]
    both = both + sign * pltpu.roll(both, tail, 1)
    middle = half // 2
    lane = lax.broadcasted_iota(jnp.int32, (middle, LANES), 1)
    packed = jnp.where(lane < tail, both[:middle], both[middle:] * sign[middle:])
    line_tail[me_q] = packed.astype(jnp.bfloat16).reshape(half_freqs, pair_rows, LANES)

    pl.semaphore_wait(barrier, len(contacts))
    buffers = [line.at[chunk] for chunk in range(chunks)] + [line_tail]
    line_waits = []
    for index, buffer in enumerate(buffers):
        for offset in range(1, qoi_count):
            pltpu.make_async_remote_copy(
                src_ref=buffer.at[me_q],
                dst_ref=buffer.at[me_q],
                send_sem=line_send.at[index],
                recv_sem=line_recv.at[index],
                device_id=(me_p, lax.rem(me_q + offset, qoi_count)),
                device_id_type=MESH,
            ).start()
        others = buffer.at[pl.ds(0, qoi_count - 1)]
        line_waits.append(
            pltpu.make_async_remote_copy(
                src_ref=others,
                dst_ref=others,
                send_sem=line_send.at[index],
                recv_sem=line_recv.at[index],
                device_id=(me_p, lax.rem(me_q + 1, qoi_count)),
                device_id_type=MESH,
            )
        )
    for contact in contacts:
        pl.semaphore_signal(known, inc=1, device_id=contact, device_id_type=MESH)

    group_copy.wait()
    slots = lax.broadcasted_iota(jnp.int32, (LANES, gauge_local), 0)
    for f in range(freq_count):
        place = (freq_count - f) % freq_count * GROUPS
        hot[f] = (slots == group_ref[...] + place).astype(jnp.float32).astype(jnp.bfloat16)

    for f in range(freq_count):
        if f % per_load == 0:
            weight_copies[f // per_load].wait()
        loose[...] = weights[f].astype(jnp.float32)
        for j in range(halves):
            columns = pl.ds(j * LANES, LANES)
            for part in range(2):
                piece = loose[
                    pl.ds(2 * j + part, param_local, stride=2 * halves), :
                ].astype(jnp.bfloat16)
                dense[f, part, :, columns] = piece[:aligned]
                dense_tail[f % half_freqs, part, pl.ds(f // half_freqs * tail, tail), columns] = (
                    piece[aligned:]
                )

    mine = me_q * param_count + me_p
    ratio = math.sqrt(GROUPS / (gauge_local * qoi_count))

    def multiply(owners, f, chunk):
        if chunk < chunks:
            left = jnp.concatenate([line[chunk, q, f] for q in owners], axis=0)
            right = [dense[f, part, chunk * LANES : (chunk + 1) * LANES, :] for part in range(2)]
        else:
            left = jnp.concatenate([line_tail[q, f % half_freqs] for q in owners], axis=0)
            lane = lax.broadcasted_iota(jnp.int32, left.shape, 1)
            left = jnp.where((lane >= tail) == (f >= half_freqs), left.astype(jnp.float32), 0.0)
            left = left.astype(jnp.bfloat16)
            right = [dense_tail[f % half_freqs, part] for part in range(2)]
        real, imag = [jnp.dot(left, side, preferred_element_type=jnp.float32) for side in right]
        results = [[], []]
        for index in range(len(owners)):
            low, mid, high = [index * pair_rows + step * sample_local for step in range(3)]
            results[0].append(real[low:mid] - imag[mid:high])
            results[1].append(imag[low:mid] + real[mid:high])
        return [jnp.concatenate(result, axis=0) for result in results]

    def add_segment(segment, values, f):
        sums = lax.dot_general(
            jnp.concatenate(values, axis=0).astype(jnp.bfloat16),
            hot[f],
            NT_DIMS,
            preferred_element_type=jnp.float32,
        )
        return sums if segment is None else segment + sums

    def rows_of(k, f, count):
        return pl.ds((k * freq_count + f) * count, count)

    def deliver(owners, product, segment):
        count = len(owners) * sample_local
        joined[pl.ds(0, 2 * count), :] = segment * ratio
        for index, q in enumerate(owners):
            for i in range(sample_local):
                shares[q * sample_local + i] = joined[
                    pl.ds(index * sample_local + i, 2, stride=count), :
                ]
        for away in reversed(range(qoi_count)):
            for q in owners:
                for i in range(sample_local):
                    target = q * sample_local + i
                    copy = pltpu.make_async_remote_copy(
                        src_ref=shares.at[target],
                        dst_ref=gathered.at[mine],
                        send_sem=share_send,
                        recv_sem=share_recv,
                        device_id=(target, lax.rem(me_q + away, qoi_count)),
                        device_id_type=MESH,
                    )
                    if away:
                        copy.start()
                    else:
                        pl.when(target != me_p)(copy.start)
        for index, q in enumerate(owners):
            for i in range(sample_local):
                for j in range(halves):
                    outgoing[q * sample_local + i, :, j * LANES : (j + 1) * LANES] = product[
                        j, pl.ds(index * sample_local + i, stripe, stride=count), :
                    ].astype(jnp.bfloat16)
        for q in owners:
            for i in range(sample_local):
                target = q * sample_local + i
                copy = pltpu.make_async_remote_copy(
                    src_ref=outgoing.at[target],
                    dst_ref=incoming.at[me_p],
                    send_sem=out_send,
                    recv_sem=out_recv,
                    device_id=(target, me_q),
                    device_id_type=MESH,
                )
                pl.when(target != me_p)(copy.start)

    segment = None
    for f in range(freq_count):
        finals = [multiply([me_q], f, chunk) for chunk in range(chunks + 1)]
        values = [sum(pieces[1:], pieces[0]) for pieces in zip(*finals)]
        for k in range(2):
            for j in range(halves):
                near[j, rows_of(k, f, sample_local), :] = values[k][:, j * LANES : (j + 1) * LANES]
        segment = add_segment(segment, values, f)
    pl.semaphore_wait(known, len(contacts))
    deliver([me_q], near, segment)

    owners = [lax.rem(me_q + offset, qoi_count) for offset in range(1, qoi_count)]
    count = len(owners) * sample_local
    segment = None
    for chunk in range(chunks + 1):
        line_waits[chunk].wait_recv()
        for f in range(freq_count):
            values = multiply(owners, f, chunk)
            for k in range(2):
                wide = []
                for j in range(halves):
                    here = values[k][:, j * LANES : (j + 1) * LANES]
                    if chunk:
                        here = here + far[j, rows_of(k, f, count), :]
                    far[j, rows_of(k, f, count), :] = here
                    wide.append(here)
                values[k] = jnp.concatenate(wide, axis=1)
            if chunk == chunks:
                segment = add_segment(segment, values, f)
    deliver(owners, far, segment)
    incoming[me_p] = outgoing[me_p]
    gathered[mine] = shares[me_p]

    aside = (lax.rem(me_p + 1, param_count), me_q)
    others = incoming.at[pl.ds(0, param_count - 1)]
    out_wait = pltpu.make_async_remote_copy(
        src_ref=others, dst_ref=others, send_sem=out_send, recv_sem=out_recv,
        device_id=aside, device_id_type=MESH,
    )
    others = gathered.at[pl.ds(0, qoi_count * param_count - 1)]
    share_wait = pltpu.make_async_remote_copy(
        src_ref=others, dst_ref=others, send_sem=share_send, recv_sem=share_recv,
        device_id=aside, device_id_type=MESH,
    )
    out_wait.wait_recv()
    total = incoming[0].astype(jnp.float32)
    for p in range(1, param_count):
        total = total + incoming[p].astype(jnp.float32)
    out_ref[...] = total.reshape(out_ref.shape)
    share_wait.wait_recv()
    final = gathered[0]
    for p in range(1, param_count * qoi_count):
        final = final + gathered[p]
    for k in range(2):
        rows = jnp.broadcast_to(final[k : k + 1], (freq_count, LANES))
        turned = pltpu.roll(rows, 0, 1, stride=GROUPS, stride_axis=0)
        seg_ref[0, k] = turned[:, :GROUPS]
    for wait in line_waits:
        wait.wait_send()
    out_wait.wait_send()
    share_wait.wait_send()


def writer(spectrum_ref, response_ref, spectrum_hbm, response_hbm, sems):
    copies = [
        pltpu.make_async_copy(spectrum_ref, spectrum_hbm, sems.at[0]),
        pltpu.make_async_copy(response_ref, response_hbm, sems.at[1]),
    ]
    for copy in copies:
        copy.start()
    for copy in copies:
        copy.wait()


def local(samples, operator_rows, block_start, gauge_group):
    sample_local, param_local, steps_count = samples.shape
    freq_count, _, _, gauge_local = operator_rows.shape
    param_count, qoi_count = lax.axis_size("param"), lax.axis_size("qoi")
    sample_total = sample_local * qoi_count
    halves = gauge_local // LANES
    depth = 2 * param_local
    stripe = 2 * freq_count
    aligned = param_local // LANES * LANES
    tail = param_local - aligned
    assert sample_total == param_count and freq_count * GROUPS == LANES
    assert 2 * tail == LANES and freq_count % LOADS == 0 and steps_count % 2 == 0
    rows = operator_rows.reshape(freq_count, param_local, 2, halves, LANES)
    rows = rows.transpose(0, 1, 3, 2, 4).reshape(freq_count, depth * halves, LANES)
    dma = pltpu.SemaphoreType.DMA
    vmem = pl.BlockSpec(memory_space=pltpu.VMEM)
    hbm = pl.BlockSpec(memory_space=pltpu.HBM)
    shapes = (
        jax.ShapeDtypeStruct((1, 2, freq_count, gauge_local), jnp.float32),
        jax.ShapeDtypeStruct((1, 2, freq_count, GROUPS), jnp.float32),
    )
    found = pl.pallas_call(
        functools.partial(kernel, param_count, qoi_count),
        out_shape=shapes,
        in_specs=[pl.BlockSpec(memory_space=pltpu.SMEM), hbm, hbm, hbm],
        out_specs=(vmem, vmem),
        scratch_shapes=[
            pltpu.VMEM((1, gauge_local), jnp.int32),
            pltpu.VMEM((steps_count, sample_local, param_local), jnp.bfloat16),
            pltpu.VMEM((4 * freq_count * sample_local, steps_count // 2 * sample_local), jnp.bfloat16),
            pltpu.VMEM((freq_count, depth * halves, LANES), jnp.bfloat16),
            pltpu.VMEM((depth * halves, LANES), jnp.float32),
            pltpu.VMEM((freq_count, 2, aligned, gauge_local), jnp.bfloat16),
            pltpu.VMEM((freq_count // 2, 2, 2 * tail, gauge_local), jnp.bfloat16),
            pltpu.VMEM((freq_count, LANES, gauge_local), jnp.bfloat16),
            pltpu.VMEM((aligned // LANES, qoi_count, freq_count, 2 * sample_local, LANES), jnp.bfloat16),
            pltpu.VMEM((qoi_count, freq_count // 2, 2 * sample_local, 2 * tail), jnp.bfloat16),
            pltpu.VMEM((halves, stripe * sample_local, LANES), jnp.float32),
            pltpu.VMEM((halves, stripe * (sample_total - sample_local), LANES), jnp.float32),
            pltpu.VMEM((sample_total, stripe, gauge_local), jnp.bfloat16),
            pltpu.VMEM((param_count, stripe, gauge_local), jnp.bfloat16),
            pltpu.VMEM((2 * sample_total, LANES), jnp.float32),
            pltpu.VMEM((sample_total, 2, LANES), jnp.float32),
            pltpu.VMEM((qoi_count * param_count, 2, LANES), jnp.float32),
            dma(()),
            dma((2,)),
            dma((LOADS,)),
            dma((aligned // LANES + 1,)),
            dma((aligned // LANES + 1,)),
            dma(()),
            dma(()),
            dma(()),
            dma(()),
            pltpu.SemaphoreType.REGULAR,
        ],
        compiler_params=pltpu.CompilerParams(
            collective_id=0, has_side_effects=True, vmem_limit_bytes=53 * 2**20
        ),
    )(
        block_start,
        pltpu.with_memory_space_constraint(gauge_group.reshape(1, gauge_local), pltpu.HBM),
        samples.transpose(2, 0, 1),
        rows,
    )
    return pl.pallas_call(
        writer,
        out_shape=shapes,
        in_specs=[vmem, vmem],
        out_specs=(pl.BlockSpec(memory_space=pl.ANY), pl.BlockSpec(memory_space=pl.ANY)),
        scratch_shapes=[dma((2,))],
    )(*[pltpu.with_memory_space_constraint(array, pltpu.VMEM) for array in found])


def solution(mesh):
    return jax.shard_map(
        local,
        mesh=mesh,
        in_specs=(P("qoi", "param", None), P(None, "param", None, "qoi"), P(), P("qoi")),
        out_specs=(P("param", None, None, "qoi"), P("param", None, None, None)),
        check_vma=False,
    )
```

time: 18.6 us -> 17.3 us (0.930)
  Pallas kernels: 17.1 us -> 15.9 us
    pallas_call x1, Pallas kernels: 16.5 us -> 15.2 us  [local(): pl.pallas_call(functools.partial(kernel, param_count, qoi_count), out_sha...]
where the time goes in v2:
time: 17.3 us; the launch traced here: 17.1 us
  Pallas kernels  15.9 us (92%)
  between operations  1.28 us (7%)
    pallas_call x1, Pallas kernels, local(): pl.pallas_call(functools.partial(kernel, param_count, qoi_count), out_sha...  15.2 us
    pallas_call x1, Pallas kernels, local(): pl.pallas_call(writer, out_shape=shapes, in_specs=[vmem, vmem], out_specs...  0.63 us

profile of v2, /device:TPU:0, one launch (start us, length us, event | category | flops | bytes accessed | tf_op | source)
XLA Modules:
  0.0 17.1 jit_solution(12191988134010123473)
XLA Ops:
  1.3 15.2 %shard_map.59 = (f32[1,2,8,256]{3,2,1,0:T(8,128)S(1)}, f32[1,2,8,16]{3,2,1,0:T(8,128)S(1)}) custom-call(s32[1]{0:T(128)S(6)} %copy.7.start_ref, s32[1,256]{1,0:T(1,128)} %bitcast.9, bf16[420,8,320]{2,1,0:T(8,128)(2,1)} %bitcast.8, bf16[8,1280,128]{2,1,0:T(8,128)(2,1)} %bitcast.7), custom_call_target="tpu_custom_call" | custom-call | tf_op jit(solution)/shard_map/pallas_call | solution.py:341
  16.5 0.6 %shard_map.60 = (f32[1,2,8,256]{3,2,1,0:T(8,128)}, f32[1,2,8,16]{3,2,1,0:T(8,128)}) custom-call(f32[1,2,8,256]{3,2,1,0:T(8,128)S(1)} %get-tuple-element.4.spectrum_ref, f32[1,2,8,16]{3,2,1,0:T(8,128)S(1)} %get-tuple-element.5.response_ref), custom_call_target="tpu_custom_call" | custom-call | tf_op jit(solution)/shard_map/pallas_call | solution.py:384

commit v3 on v2

--- a/solution.py
+++ b/solution.py
@@ -10,7 +10,7 @@
 
 GROUPS = 16
 LANES = 128
-LOADS = 4
+LOADS = 2
 MESH = pl.DeviceIdType.MESH
 NT_DIMS = (((1,), (1,)), ((), ()))
 
@@ -43,7 +43,7 @@
 def kernel(
     param_count, qoi_count, start_ref, group_hbm, samples_hbm, rows_hbm,
     out_ref, seg_ref,
-    group_ref, samples, table, weights, loose, dense, dense_tail, hot, line, line_tail, near, far, outgoing, incoming, joined, shares, gathered,
+    group_ref, samples, table, weights, loose, dense, dense_tail, hot, line, near, far, outgoing, incoming, joined, shares, gathered,
     group_sem, samples_sem, weights_sem, line_send, line_recv, out_send, out_recv, share_send, share_recv, known,
 ):
     steps_count, sample_local, param_local = samples.shape
@@ -72,13 +72,8 @@
                     (base + lax.rem(me_p + turn, inner), lax.rem(me_q + other, qoi_count))
                 )
     barrier = pltpu.get_barrier_semaphore()
-    spans = [pl.ds(0, half_steps), pl.ds(half_steps, half_steps)]
-    sample_copies = [
-        pltpu.make_async_copy(samples_hbm.at[span], samples.at[span], samples_sem.at[part])
-        for part, span in enumerate(spans)
-    ]
-    for copy in sample_copies:
-        copy.start()
+    sample_copy = pltpu.make_async_copy(samples_hbm, samples, samples_sem)
+    sample_copy.start()
     for contact in contacts:
         pl.semaphore_signal(barrier, inc=1, device_id=contact, device_id_type=MESH)
     group_copy = pltpu.make_async_copy(group_hbm, group_ref, group_sem)
@@ -93,64 +88,70 @@
     start = start_ref[0]
     build_table(start, freq_count, steps_count, half_steps, sample_local, table)
 
+    group_copy.wait()
+    slots = lax.broadcasted_iota(jnp.int32, (LANES, gauge_local), 0)
+    for f in range(freq_count):
+        place = (freq_count - f) % freq_count * GROUPS
+        hot[f] = (slots == group_ref[...] + place).astype(jnp.float32).astype(jnp.bfloat16)
+
+    sample_copy.wait()
+    for copy in weight_copies:
+        copy.start()
+    pl.semaphore_wait(barrier, len(contacts))
+    for contact in contacts:
+        pl.semaphore_signal(known, inc=1, device_id=contact, device_id_type=MESH)
+
+    def send_line(first, count, index):
+        picked = pl.ds(first, count)
+        for offset in range(1, qoi_count):
+            pltpu.make_async_remote_copy(
+                src_ref=line.at[me_q, picked],
+                dst_ref=line.at[me_q, picked],
+                send_sem=line_send,
+                recv_sem=line_recv.at[index],
+                device_id=(me_p, lax.rem(me_q + offset, qoi_count)),
+                device_id_type=MESH,
+            ).start()
+
+    def wait_line(first, count, index):
+        others = line.at[pl.ds(0, qoi_count - 1), pl.ds(first, count)]
+        return pltpu.make_async_remote_copy(
+            src_ref=others,
+            dst_ref=others,
+            send_sem=line_send,
+            recv_sem=line_recv.at[index],
+            device_id=(me_p, lax.rem(me_q + 1, qoi_count)),
+            device_id_type=MESH,
+        )
+
     turns = table[...]
-    blocks, sides = [], []
     half = freq_count * pair_rows
+    sides, ends = [], []
     for part in range(2):
-        sample_copies[part].wait()
-        if part == 0:
-            for copy in weight_copies:
-                copy.start()
-        block = samples[spans[part]].reshape(half_steps * sample_local, param_local)
+        block = samples[pl.ds(part * half_steps, half_steps)]
+        block = block.reshape(half_steps * sample_local, param_local)
         both = jnp.dot(turns, block[:, :aligned], preferred_element_type=jnp.float32)
         sides.append(both[:half] + both[half:])
-        blocks.append(block[:, aligned:])
+        ends.append(block[:, aligned:])
     odd = lax.rem(start + lax.broadcasted_iota(jnp.int32, (half, LANES), 0) // pair_rows, 2)
     sign = 1.0 - 2.0 * odd.astype(jnp.float32)
     for chunk in range(chunks):
         columns = slice(chunk * LANES, (chunk + 1) * LANES)
         spectrum = sides[0][:, columns] + sign * sides[1][:, columns]
-        line[chunk, me_q] = spectrum.astype(jnp.bfloat16).reshape(freq_count, pair_rows, LANES)
-    both = jnp.dot(turns, jnp.concatenate(blocks, axis=1), preferred_element_type=jnp.float32)
+        line[me_q, chunk * freq_count : (chunk + 1) * freq_count] = spectrum.astype(
+            jnp.bfloat16
+        ).reshape(freq_count, pair_rows, LANES)
+        send_line(chunk * freq_count, freq_count, chunk)
+    both = jnp.dot(turns, jnp.concatenate(ends, axis=1), preferred_element_type=jnp.float32)
     both = both[:half] + both[half:]
     both = both + sign * pltpu.roll(both, tail, 1)
     middle = half // 2
     lane = lax.broadcasted_iota(jnp.int32, (middle, LANES), 1)
     packed = jnp.where(lane < tail, both[:middle], both[middle:] * sign[middle:])
-    line_tail[me_q] = packed.astype(jnp.bfloat16).reshape(half_freqs, pair_rows, LANES)
-
-    pl.semaphore_wait(barrier, len(contacts))
-    buffers = [line.at[chunk] for chunk in range(chunks)] + [line_tail]
-    line_waits = []
-    for index, buffer in enumerate(buffers):
-        for offset in range(1, qoi_count):
-            pltpu.make_async_remote_copy(
-                src_ref=buffer.at[me_q],
-                dst_ref=buffer.at[me_q],
-                send_sem=line_send.at[index],
-                recv_sem=line_recv.at[index],
-                device_id=(me_p, lax.rem(me_q + offset, qoi_count)),
-                device_id_type=MESH,
-            ).start()
-        others = buffer.at[pl.ds(0, qoi_count - 1)]
-        line_waits.append(
-            pltpu.make_async_remote_copy(
-                src_ref=others,
-                dst_ref=others,
-                send_sem=line_send.at[index],
-                recv_sem=line_recv.at[index],
-                device_id=(me_p, lax.rem(me_q + 1, qoi_count)),
-                device_id_type=MESH,
-            )
-        )
-    for contact in contacts:
-        pl.semaphore_signal(known, inc=1, device_id=contact, device_id_type=MESH)
-
-    group_copy.wait()
-    slots = lax.broadcasted_iota(jnp.int32, (LANES, gauge_local), 0)
-    for f in range(freq_count):
-        place = (freq_count - f) % freq_count * GROUPS
-        hot[f] = (slots == group_ref[...] + place).astype(jnp.float32).astype(jnp.bfloat16)
+    line[me_q, chunks * freq_count :] = packed.astype(jnp.bfloat16).reshape(
+        half_freqs, pair_rows, LANES
+    )
+    send_line(chunks * freq_count, half_freqs, chunks)
 
     for f in range(freq_count):
         if f % per_load == 0:
@@ -172,10 +173,12 @@
 
     def multiply(owners, f, chunk):
         if chunk < chunks:
-            left = jnp.concatenate([line[chunk, q, f] for q in owners], axis=0)
+            left = jnp.concatenate([line[q, chunk * freq_count + f] for q in owners], axis=0)
             right = [dense[f, part, chunk * LANES : (chunk + 1) * LANES, :] for part in range(2)]
         else:
-            left = jnp.concatenate([line_tail[q, f % half_freqs] for q in owners], axis=0)
+            left = jnp.concatenate(
+                [line[q, chunks * freq_count + f % half_freqs] for q in owners], axis=0
+            )
             lane = lax.broadcasted_iota(jnp.int32, left.shape, 1)
             left = jnp.where((lane >= tail) == (f >= half_freqs), left.astype(jnp.float32), 0.0)
             left = left.astype(jnp.bfloat16)
@@ -258,7 +261,8 @@
     count = len(owners) * sample_local
     segment = None
     for chunk in range(chunks + 1):
-        line_waits[chunk].wait_recv()
+        rows = freq_count if chunk < chunks else half_freqs
+        wait_line(chunk * freq_count, rows, chunk).wait_recv()
         for f in range(freq_count):
             values = multiply(owners, f, chunk)
             for k in range(2):
@@ -300,8 +304,7 @@
         rows = jnp.broadcast_to(final[k : k + 1], (freq_count, LANES))
         turned = pltpu.roll(rows, 0, 1, stride=GROUPS, stride_axis=0)
         seg_ref[0, k] = turned[:, :GROUPS]
-    for wait in line_waits:
-        wait.wait_send()
+    wait_line(0, chunks * freq_count + half_freqs, 0).wait_send()
     out_wait.wait_send()
     share_wait.wait_send()
 
@@ -352,8 +355,10 @@
             pltpu.VMEM((freq_count, 2, aligned, gauge_local), jnp.bfloat16),
             pltpu.VMEM((freq_count // 2, 2, 2 * tail, gauge_local), jnp.bfloat16),
             pltpu.VMEM((freq_count, LANES, gauge_local), jnp.bfloat16),
-            pltpu.VMEM((aligned // LANES, qoi_count, freq_count, 2 * sample_local, LANES), jnp.bfloat16),
-            pltpu.VMEM((qoi_count, freq_count // 2, 2 * sample_local, 2 * tail), jnp.bfloat16),
+            pltpu.VMEM(
+                (qoi_count, aligned // LANES * freq_count + freq_count // 2, 2 * sample_local, LANES),
+                jnp.bfloat16,
+            ),
             pltpu.VMEM((halves, stripe * sample_local, LANES), jnp.float32),
             pltpu.VMEM((halves, stripe * (sample_total - sample_local), LANES), jnp.float32),
             pltpu.VMEM((sample_total, stripe, gauge_local), jnp.bfloat16),
@@ -362,9 +367,9 @@
             pltpu.VMEM((sample_total, 2, LANES), jnp.float32),
             pltpu.VMEM((qoi_count * param_count, 2, LANES), jnp.float32),
             dma(()),
-            dma((2,)),
+            dma(()),
             dma((LOADS,)),
-            dma((aligned // LANES + 1,)),
+            dma(()),
             dma((aligned // LANES + 1,)),
             dma(()),
             dma(()),

time: 17.3 us -> 17 us (0.983)
  Pallas kernels: 15.9 us -> 15.6 us
    pallas_call x1, Pallas kernels: 15.2 us -> 14.9 us  [local(): pl.pallas_call(functools.partial(kernel, param_count, qoi_count), out_sha...]
where the time goes in v3:
time: 17 us; the launch traced here: 16.8 us
  Pallas kernels  15.6 us (92%)
  between operations  1.28 us (8%)
    pallas_call x1, Pallas kernels, local(): pl.pallas_call(functools.partial(kernel, param_count, qoi_count), out_sha...  14.9 us
    pallas_call x1, Pallas kernels, local(): pl.pallas_call(writer, out_shape=shapes, in_specs=[vmem, vmem], out_specs...  0.63 us

profile of v3, /device:TPU:0, one launch (start us, length us, event | category | flops | bytes accessed | tf_op | source)
XLA Modules:
  0.0 16.8 jit_solution(15412304742359854835)
XLA Ops:
  1.3 14.9 %shard_map.59 = (f32[1,2,8,256]{3,2,1,0:T(8,128)S(1)}, f32[1,2,8,16]{3,2,1,0:T(8,128)S(1)}) custom-call(s32[1]{0:T(128)S(6)} %copy.7.start_ref, s32[1,256]{1,0:T(1,128)} %bitcast.9, bf16[420,8,320]{2,1,0:T(8,128)(2,1)} %bitcast.8, bf16[8,1280,128]{2,1,0:T(8,128)(2,1)} %bitcast.7), custom_call_target="tpu_custom_call" | custom-call | tf_op jit(solution)/shard_map/pallas_call | solution.py:344
  16.2 0.6 %shard_map.60 = (f32[1,2,8,256]{3,2,1,0:T(8,128)}, f32[1,2,8,16]{3,2,1,0:T(8,128)}) custom-call(f32[1,2,8,256]{3,2,1,0:T(8,128)S(1)} %get-tuple-element.4.spectrum_ref, f32[1,2,8,16]{3,2,1,0:T(8,128)S(1)} %get-tuple-element.5.response_ref), custom_call_target="tpu_custom_call" | custom-call | tf_op jit(solution)/shard_map/pallas_call | solution.py:389

commit v4 on v3

--- a/solution.py
+++ b/solution.py
@@ -72,12 +72,12 @@
                     (base + lax.rem(me_p + turn, inner), lax.rem(me_q + other, qoi_count))
                 )
     barrier = pltpu.get_barrier_semaphore()
+    group_copy = pltpu.make_async_copy(group_hbm, group_ref, group_sem)
+    group_copy.start()
     sample_copy = pltpu.make_async_copy(samples_hbm, samples, samples_sem)
     sample_copy.start()
     for contact in contacts:
         pl.semaphore_signal(barrier, inc=1, device_id=contact, device_id_type=MESH)
-    group_copy = pltpu.make_async_copy(group_hbm, group_ref, group_sem)
-    group_copy.start()
     per_load = freq_count // LOADS
     loads = [pl.ds(load * per_load, per_load) for load in range(LOADS)]
     weight_copies = [
@@ -87,6 +87,8 @@
 
     start = start_ref[0]
     build_table(start, freq_count, steps_count, half_steps, sample_local, table)
+    for copy in weight_copies:
+        copy.start()
 
     group_copy.wait()
     slots = lax.broadcasted_iota(jnp.int32, (LANES, gauge_local), 0)
@@ -95,11 +97,6 @@
         hot[f] = (slots == group_ref[...] + place).astype(jnp.float32).astype(jnp.bfloat16)
 
     sample_copy.wait()
-    for copy in weight_copies:
-        copy.start()
-    pl.semaphore_wait(barrier, len(contacts))
-    for contact in contacts:
-        pl.semaphore_signal(known, inc=1, device_id=contact, device_id_type=MESH)
 
     def send_line(first, count, index):
         picked = pl.ds(first, count)
@@ -135,6 +132,7 @@
         ends.append(block[:, aligned:])
     odd = lax.rem(start + lax.broadcasted_iota(jnp.int32, (half, LANES), 0) // pair_rows, 2)
     sign = 1.0 - 2.0 * odd.astype(jnp.float32)
+    pl.semaphore_wait(barrier, len(contacts))
     for chunk in range(chunks):
         columns = slice(chunk * LANES, (chunk + 1) * LANES)
         spectrum = sides[0][:, columns] + sign * sides[1][:, columns]
@@ -142,6 +140,8 @@
             jnp.bfloat16
         ).reshape(freq_count, pair_rows, LANES)
         send_line(chunk * freq_count, freq_count, chunk)
+    for contact in contacts:
+        pl.semaphore_signal(known, inc=1, device_id=contact, device_id_type=MESH)
     both = jnp.dot(turns, jnp.concatenate(ends, axis=1), preferred_element_type=jnp.float32)
     both = both[:half] + both[half:]
     both = both + sign * pltpu.roll(both, tail, 1)
@@ -246,37 +246,29 @@
                 )
                 pl.when(target != me_p)(copy.start)
 
-    segment = None
-    for f in range(freq_count):
-        finals = [multiply([me_q], f, chunk) for chunk in range(chunks + 1)]
-        values = [sum(pieces[1:], pieces[0]) for pieces in zip(*finals)]
-        for k in range(2):
-            for j in range(halves):
-                near[j, rows_of(k, f, sample_local), :] = values[k][:, j * LANES : (j + 1) * LANES]
-        segment = add_segment(segment, values, f)
-    pl.semaphore_wait(known, len(contacts))
-    deliver([me_q], near, segment)
-
-    owners = [lax.rem(me_q + offset, qoi_count) for offset in range(1, qoi_count)]
-    count = len(owners) * sample_local
-    segment = None
-    for chunk in range(chunks + 1):
-        rows = freq_count if chunk < chunks else half_freqs
-        wait_line(chunk * freq_count, rows, chunk).wait_recv()
-        for f in range(freq_count):
-            values = multiply(owners, f, chunk)
-            for k in range(2):
-                wide = []
-                for j in range(halves):
-                    here = values[k][:, j * LANES : (j + 1) * LANES]
-                    if chunk:
-                        here = here + far[j, rows_of(k, f, count), :]
-                    far[j, rows_of(k, f, count), :] = here
-                    wide.append(here)
-                values[k] = jnp.concatenate(wide, axis=1)
-            if chunk == chunks:
-                segment = add_segment(segment, values, f)
-    deliver(owners, far, segment)
+    for owners, product in (([0], near), (list(range(1, qoi_count)), far)):
+        count = len(owners) * sample_local
+        segment = None
+        for chunk in range(chunks + 1):
+            rows = freq_count if chunk < chunks else half_freqs
+            line_wait = wait_line(chunk * freq_count, rows, chunk)
+            pl.when(me_q != 0 if owners == [0] else me_q == 0)(line_wait.wait_recv)
+            for f in range(freq_count):
+                values = multiply(owners, f, chunk)
+                for k in range(2):
+                    wide = []
+                    for j in range(halves):
+                        here = values[k][:, j * LANES : (j + 1) * LANES]
+                        if chunk:
+                            here = here + product[j, rows_of(k, f, count), :]
+                        product[j, rows_of(k, f, count), :] = here
+                        wide.append(here)
+                    values[k] = jnp.concatenate(wide, axis=1)
+                if chunk == chunks:
+                    segment = add_segment(segment, values, f)
+        if owners == [0]:
+            pl.semaphore_wait(known, len(contacts))
+        deliver(owners, product, segment)
     incoming[me_p] = outgoing[me_p]
     gathered[mine] = shares[me_p]
 

time: 17 us -> 16.9 us (level)
  Pallas kernels: 15.6 us -> 15.4 us
where the time goes in v4:
time: 16.9 us; the launch traced here: 16.7 us
  Pallas kernels  15.4 us (91%)
  between operations  1.28 us (8%)
    pallas_call x1, Pallas kernels, local(): pl.pallas_call(functools.partial(kernel, param_count, qoi_count), out_sha...  14.8 us
    pallas_call x1, Pallas kernels, local(): pl.pallas_call(writer, out_shape=shapes, in_specs=[vmem, vmem], out_specs...  0.63 us

profile of v4, /device:TPU:0, one launch (start us, length us, event | category | flops | bytes accessed | tf_op | source)
XLA Modules:
  0.0 16.7 jit_solution(11457867733093520311)
XLA Ops:
  1.3 14.8 %shard_map.59 = (f32[1,2,8,256]{3,2,1,0:T(8,128)S(1)}, f32[1,2,8,16]{3,2,1,0:T(8,128)S(1)}) custom-call(s32[1]{0:T(128)S(6)} %copy.7.start_ref, s32[1,256]{1,0:T(1,128)} %bitcast.9, bf16[420,8,320]{2,1,0:T(8,128)(2,1)} %bitcast.8, bf16[8,1280,128]{2,1,0:T(8,128)(2,1)} %bitcast.7), custom_call_target="tpu_custom_call" | custom-call | tf_op jit(solution)/shard_map/pallas_call | solution.py:336
  16.1 0.6 %shard_map.60 = (f32[1,2,8,256]{3,2,1,0:T(8,128)}, f32[1,2,8,16]{3,2,1,0:T(8,128)}) custom-call(f32[1,2,8,256]{3,2,1,0:T(8,128)S(1)} %get-tuple-element.4.spectrum_ref, f32[1,2,8,16]{3,2,1,0:T(8,128)S(1)} %get-tuple-element.5.response_ref), custom_call_target="tpu_custom_call" | custom-call | tf_op jit(solution)/shard_map/pallas_call | solution.py:381

commit v5 on v4

--- a/solution.py
+++ b/solution.py
@@ -74,8 +74,13 @@
     barrier = pltpu.get_barrier_semaphore()
     group_copy = pltpu.make_async_copy(group_hbm, group_ref, group_sem)
     group_copy.start()
-    sample_copy = pltpu.make_async_copy(samples_hbm, samples, samples_sem)
-    sample_copy.start()
+    lanes = [pl.ds(0, aligned), pl.ds(aligned, tail)]
+    sample_copies = [
+        pltpu.make_async_copy(samples_hbm.at[:, :, lane], samples.at[:, :, lane], samples_sem.at[part])
+        for part, lane in enumerate(lanes)
+    ]
+    for copy in sample_copies:
+        copy.start()
     for contact in contacts:
         pl.semaphore_signal(barrier, inc=1, device_id=contact, device_id_type=MESH)
     per_load = freq_count // LOADS
@@ -90,13 +95,7 @@
     for copy in weight_copies:
         copy.start()
 
-    group_copy.wait()
-    slots = lax.broadcasted_iota(jnp.int32, (LANES, gauge_local), 0)
-    for f in range(freq_count):
-        place = (freq_count - f) % freq_count * GROUPS
-        hot[f] = (slots == group_ref[...] + place).astype(jnp.float32).astype(jnp.bfloat16)
-
-    sample_copy.wait()
+    sample_copies[0].wait()
 
     def send_line(first, count, index):
         picked = pl.ds(first, count)
@@ -125,11 +124,10 @@
     half = freq_count * pair_rows
     sides, ends = [], []
     for part in range(2):
-        block = samples[pl.ds(part * half_steps, half_steps)]
-        block = block.reshape(half_steps * sample_local, param_local)
-        both = jnp.dot(turns, block[:, :aligned], preferred_element_type=jnp.float32)
+        block = samples[pl.ds(part * half_steps, half_steps), :, pl.ds(0, aligned)]
+        block = block.reshape(half_steps * sample_local, aligned)
+        both = jnp.dot(turns, block, preferred_element_type=jnp.float32)
         sides.append(both[:half] + both[half:])
-        ends.append(block[:, aligned:])
     odd = lax.rem(start + lax.broadcasted_iota(jnp.int32, (half, LANES), 0) // pair_rows, 2)
     sign = 1.0 - 2.0 * odd.astype(jnp.float32)
     pl.semaphore_wait(barrier, len(contacts))
@@ -142,6 +140,10 @@
         send_line(chunk * freq_count, freq_count, chunk)
     for contact in contacts:
         pl.semaphore_signal(known, inc=1, device_id=contact, device_id_type=MESH)
+    sample_copies[1].wait()
+    for part in range(2):
+        block = samples[pl.ds(part * half_steps, half_steps), :, pl.ds(aligned, tail)]
+        ends.append(block.reshape(half_steps * sample_local, tail))
     both = jnp.dot(turns, jnp.concatenate(ends, axis=1), preferred_element_type=jnp.float32)
     both = both[:half] + both[half:]
     both = both + sign * pltpu.roll(both, tail, 1)
@@ -152,6 +154,12 @@
         half_freqs, pair_rows, LANES
     )
     send_line(chunks * freq_count, half_freqs, chunks)
+
+    group_copy.wait()
+    slots = lax.broadcasted_iota(jnp.int32, (LANES, gauge_local), 0)
+    for f in range(freq_count):
+        place = (freq_count - f) % freq_count * GROUPS
+        hot[f] = (slots == group_ref[...] + place).astype(jnp.float32).astype(jnp.bfloat16)
 
     for f in range(freq_count):
         if f % per_load == 0:
@@ -359,7 +367,7 @@
             pltpu.VMEM((sample_total, 2, LANES), jnp.float32),
             pltpu.VMEM((qoi_count * param_count, 2, LANES), jnp.float32),
             dma(()),
-            dma(()),
+            dma((2,)),
             dma((LOADS,)),
             dma(()),
             dma((aligned // LANES + 1,)),

time: 16.9 us -> 16.5 us (0.976)
  Pallas kernels: 15.4 us -> 15 us
    pallas_call x1, Pallas kernels: 14.8 us -> 14.4 us  [local(): pl.pallas_call(functools.partial(kernel, param_count, qoi_count), out_sha...]
where the time goes in v5:
time: 16.5 us; the launch traced here: 16.3 us
  Pallas kernels  15 us (91%)
  between operations  1.28 us (8%)
    pallas_call x1, Pallas kernels, local(): pl.pallas_call(functools.partial(kernel, param_count, qoi_count), out_sha...  14.4 us
    pallas_call x1, Pallas kernels, local(): pl.pallas_call(writer, out_shape=shapes, in_specs=[vmem, vmem], out_specs...  0.63 us

profile of v5, /device:TPU:0, one launch (start us, length us, event | category | flops | bytes accessed | tf_op | source)
XLA Modules:
  0.0 16.3 jit_solution(11536145271746424043)
XLA Ops:
  1.3 14.4 %shard_map.59 = (f32[1,2,8,256]{3,2,1,0:T(8,128)S(1)}, f32[1,2,8,16]{3,2,1,0:T(8,128)S(1)}) custom-call(s32[1]{0:T(128)S(6)} %copy.7.start_ref, s32[1,256]{1,0:T(1,128)} %bitcast.9, bf16[420,8,320]{2,1,0:T(8,128)(2,1)} %bitcast.8, bf16[8,1280,128]{2,1,0:T(8,128)(2,1)} %bitcast.7), custom_call_target="tpu_custom_call" | custom-call | tf_op jit(solution)/shard_map/pallas_call | solution.py:344
  15.7 0.6 %shard_map.60 = (f32[1,2,8,256]{3,2,1,0:T(8,128)}, f32[1,2,8,16]{3,2,1,0:T(8,128)}) custom-call(f32[1,2,8,256]{3,2,1,0:T(8,128)S(1)} %get-tuple-element.4.spectrum_ref, f32[1,2,8,16]{3,2,1,0:T(8,128)S(1)} %get-tuple-element.5.response_ref), custom_call_target="tpu_custom_call" | custom-call | tf_op jit(solution)/shard_map/pallas_call | solution.py:389

commit v6 on v5

--- a/solution.py
+++ b/solution.py
@@ -43,7 +43,7 @@
 def kernel(
     param_count, qoi_count, start_ref, group_hbm, samples_hbm, rows_hbm,
     out_ref, seg_ref,
-    group_ref, samples, table, weights, loose, dense, dense_tail, hot, line, near, far, outgoing, incoming, joined, shares, gathered,
+    group_ref, samples, table, weights, loose, dense, dense_tail, grouped, grouped_tail, hot, line, near, far, outgoing, incoming, joined, shares, gathered,
     group_sem, samples_sem, weights_sem, line_send, line_recv, out_send, out_recv, share_send, share_recv, known,
 ):
     steps_count, sample_local, param_local = samples.shape
@@ -161,6 +161,10 @@
         place = (freq_count - f) % freq_count * GROUPS
         hot[f] = (slots == group_ref[...] + place).astype(jnp.float32).astype(jnp.bfloat16)
 
+    def group_sums(right, f):
+        sums = lax.dot_general(right, hot[f], NT_DIMS, preferred_element_type=jnp.float32)
+        return sums.astype(jnp.bfloat16)
+
     for f in range(freq_count):
         if f % per_load == 0:
             weight_copies[f // per_load].wait()
@@ -175,9 +179,26 @@
                 dense_tail[f % half_freqs, part, pl.ds(f // half_freqs * tail, tail), columns] = (
                     piece[aligned:]
                 )
+        for part in range(2):
+            ending = pl.ds(f // half_freqs * tail, tail)
+            grouped_tail[f % half_freqs, part, ending] = group_sums(
+                dense_tail[f % half_freqs, part, ending], f
+            )
+            sums = group_sums(dense[f, part], f)
+            for chunk in range(chunks):
+                grouped[chunk, part, f] = sums[chunk * LANES : (chunk + 1) * LANES]
 
     mine = me_q * param_count + me_p
     ratio = math.sqrt(GROUPS / (gauge_local * qoi_count))
+
+    def combine(sides):
+        real, imag = sides
+        results = [[], []]
+        for index in range(real.shape[0] // pair_rows):
+            low, mid, high = [index * pair_rows + step * sample_local for step in range(3)]
+            results[0].append(real[low:mid] - imag[mid:high])
+            results[1].append(imag[low:mid] + real[mid:high])
+        return [jnp.concatenate(result, axis=0) for result in results]
 
     def multiply(owners, f, chunk):
         if chunk < chunks:
@@ -191,27 +212,34 @@
             left = jnp.where((lane >= tail) == (f >= half_freqs), left.astype(jnp.float32), 0.0)
             left = left.astype(jnp.bfloat16)
             right = [dense_tail[f % half_freqs, part] for part in range(2)]
-        real, imag = [jnp.dot(left, side, preferred_element_type=jnp.float32) for side in right]
-        results = [[], []]
-        for index in range(len(owners)):
-            low, mid, high = [index * pair_rows + step * sample_local for step in range(3)]
-            results[0].append(real[low:mid] - imag[mid:high])
-            results[1].append(imag[low:mid] + real[mid:high])
-        return [jnp.concatenate(result, axis=0) for result in results]
-
-    def add_segment(segment, values, f):
-        sums = lax.dot_general(
-            jnp.concatenate(values, axis=0).astype(jnp.bfloat16),
-            hot[f],
-            NT_DIMS,
-            preferred_element_type=jnp.float32,
+        return combine(
+            [jnp.dot(left, side, preferred_element_type=jnp.float32) for side in right]
         )
-        return sums if segment is None else segment + sums
+
+    def group_products(owners, chunk):
+        tiles = freq_count if chunk < chunks else half_freqs
+        left = jnp.concatenate(
+            [
+                jnp.concatenate([line[q, chunk * freq_count + tile] for tile in range(tiles)], axis=1)
+                for q in owners
+            ],
+            axis=0,
+        )
+        right = grouped.at[chunk] if chunk < chunks else grouped_tail
+        results = []
+        for part in range(2):
+            if chunk < chunks:
+                side = right[part]
+            else:
+                side = jnp.stack([right[tile, part] for tile in range(tiles)], axis=0)
+            side = side.reshape(tiles * LANES, LANES)
+            results.append(jnp.dot(left, side, preferred_element_type=jnp.float32))
+        return results
 
     def rows_of(k, f, count):
         return pl.ds((k * freq_count + f) * count, count)
 
-    def deliver(owners, product, segment):
+    def deliver_shares(owners, segment):
         count = len(owners) * sample_local
         joined[pl.ds(0, 2 * count), :] = segment * ratio
         for index, q in enumerate(owners):
@@ -235,6 +263,9 @@
                         copy.start()
                     else:
                         pl.when(target != me_p)(copy.start)
+
+    def deliver_blocks(owners, product):
+        count = len(owners) * sample_local
         for index, q in enumerate(owners):
             for i in range(sample_local):
                 for j in range(halves):
@@ -256,27 +287,25 @@
 
     for owners, product in (([0], near), (list(range(1, qoi_count)), far)):
         count = len(owners) * sample_local
-        segment = None
+        totals = None
         for chunk in range(chunks + 1):
             rows = freq_count if chunk < chunks else half_freqs
             line_wait = wait_line(chunk * freq_count, rows, chunk)
             pl.when(me_q != 0 if owners == [0] else me_q == 0)(line_wait.wait_recv)
+            sums = group_products(owners, chunk)
+            totals = sums if totals is None else [a + b for a, b in zip(totals, sums)]
+            if chunk == chunks:
+                if owners == [0]:
+                    pl.semaphore_wait(known, len(contacts))
+                deliver_shares(owners, jnp.concatenate(combine(totals), axis=0))
             for f in range(freq_count):
-                values = multiply(owners, f, chunk)
-                for k in range(2):
-                    wide = []
+                for k, value in enumerate(multiply(owners, f, chunk)):
                     for j in range(halves):
-                        here = values[k][:, j * LANES : (j + 1) * LANES]
+                        here = value[:, j * LANES : (j + 1) * LANES]
                         if chunk:
                             here = here + product[j, rows_of(k, f, count), :]
                         product[j, rows_of(k, f, count), :] = here
-                        wide.append(here)
-                    values[k] = jnp.concatenate(wide, axis=1)
-                if chunk == chunks:
-                    segment = add_segment(segment, values, f)
-        if owners == [0]:
-            pl.semaphore_wait(known, len(contacts))
-        deliver(owners, product, segment)
+        deliver_blocks(owners, product)
     incoming[me_p] = outgoing[me_p]
     gathered[mine] = shares[me_p]
 
@@ -354,6 +383,8 @@
             pltpu.VMEM((depth * halves, LANES), jnp.float32),
             pltpu.VMEM((freq_count, 2, aligned, gauge_local), jnp.bfloat16),
             pltpu.VMEM((freq_count // 2, 2, 2 * tail, gauge_local), jnp.bfloat16),
+            pltpu.VMEM((aligned // LANES, 2, freq_count, LANES, LANES), jnp.bfloat16),
+            pltpu.VMEM((freq_count // 2, 2, 2 * tail, LANES), jnp.bfloat16),
             pltpu.VMEM((freq_count, LANES, gauge_local), jnp.bfloat16),
             pltpu.VMEM(
                 (qoi_count, aligned // LANES * freq_count + freq_count // 2, 2 * sample_local, LANES),

time: 16.5 us -> 16.3 us (0.988)
  Pallas kernels: 15 us -> 14.8 us
    pallas_call x1, Pallas kernels: 14.4 us -> 14.2 us  [local(): pl.pallas_call(functools.partial(kernel, param_count, qoi_count), out_sha...]
where the time goes in v6:
time: 16.3 us; the launch traced here: 16.1 us
  Pallas kernels  14.8 us (91%)
  between operations  1.28 us (8%)
    pallas_call x1, Pallas kernels, local(): pl.pallas_call(functools.partial(kernel, param_count, qoi_count), out_sha...  14.2 us
    pallas_call x1, Pallas kernels, local(): pl.pallas_call(writer, out_shape=shapes, in_specs=[vmem, vmem], out_specs...  0.63 us

profile of v6, /device:TPU:0, one launch (start us, length us, event | category | flops | bytes accessed | tf_op | source)
XLA Modules:
  0.0 16.1 jit_solution(9523863468366527447)
XLA Ops:
  1.3 14.2 %shard_map.59 = (f32[1,2,8,256]{3,2,1,0:T(8,128)S(1)}, f32[1,2,8,16]{3,2,1,0:T(8,128)S(1)}) custom-call(s32[1]{0:T(128)S(6)} %copy.7.start_ref, s32[1,256]{1,0:T(1,128)} %bitcast.9, bf16[420,8,320]{2,1,0:T(8,128)(2,1)} %bitcast.8, bf16[8,1280,128]{2,1,0:T(8,128)(2,1)} %bitcast.7), custom_call_target="tpu_custom_call" | custom-call | tf_op jit(solution)/shard_map/pallas_call | solution.py:373
  15.5 0.6 %shard_map.60 = (f32[1,2,8,256]{3,2,1,0:T(8,128)}, f32[1,2,8,16]{3,2,1,0:T(8,128)}) custom-call(f32[1,2,8,256]{3,2,1,0:T(8,128)S(1)} %get-tuple-element.4.spectrum_ref, f32[1,2,8,16]{3,2,1,0:T(8,128)S(1)} %get-tuple-element.5.response_ref), custom_call_target="tpu_custom_call" | custom-call | tf_op jit(solution)/shard_map/pallas_call | solution.py:420

commit v7 on v6

--- a/solution.py
+++ b/solution.py
@@ -161,32 +161,20 @@
         place = (freq_count - f) % freq_count * GROUPS
         hot[f] = (slots == group_ref[...] + place).astype(jnp.float32).astype(jnp.bfloat16)
 
-    def group_sums(right, f):
-        sums = lax.dot_general(right, hot[f], NT_DIMS, preferred_element_type=jnp.float32)
-        return sums.astype(jnp.bfloat16)
-
     for f in range(freq_count):
         if f % per_load == 0:
             weight_copies[f // per_load].wait()
         loose[...] = weights[f].astype(jnp.float32)
-        for j in range(halves):
-            columns = pl.ds(j * LANES, LANES)
-            for part in range(2):
-                piece = loose[
-                    pl.ds(2 * j + part, param_local, stride=2 * halves), :
-                ].astype(jnp.bfloat16)
-                dense[f, part, :, columns] = piece[:aligned]
-                dense_tail[f % half_freqs, part, pl.ds(f // half_freqs * tail, tail), columns] = (
-                    piece[aligned:]
-                )
         for part in range(2):
-            ending = pl.ds(f // half_freqs * tail, tail)
-            grouped_tail[f % half_freqs, part, ending] = group_sums(
-                dense_tail[f % half_freqs, part, ending], f
-            )
-            sums = group_sums(dense[f, part], f)
-            for chunk in range(chunks):
-                grouped[chunk, part, f] = sums[chunk * LANES : (chunk + 1) * LANES]
+            piece = jnp.concatenate(
+                [
+                    loose[pl.ds(2 * j + part, param_local, stride=2 * halves), :]
+                    for j in range(halves)
+                ],
+                axis=1,
+            ).astype(jnp.bfloat16)
+            dense[f, part] = piece[:aligned]
+            dense_tail[f % half_freqs, part, pl.ds(f // half_freqs * tail, tail)] = piece[aligned:]
 
     mine = me_q * param_count + me_p
     ratio = math.sqrt(GROUPS / (gauge_local * qoi_count))
@@ -215,6 +203,24 @@
         return combine(
             [jnp.dot(left, side, preferred_element_type=jnp.float32) for side in right]
         )
+
+    def build_grouped():
+        for f in range(freq_count):
+            ending = pl.ds(f // half_freqs * tail, tail)
+            rows = []
+            for part in range(2):
+                rows += [dense[f, part], dense_tail[f % half_freqs, part, ending]]
+            sums = lax.dot_general(
+                jnp.concatenate(rows, axis=0), hot[f], NT_DIMS, preferred_element_type=jnp.float32
+            ).astype(jnp.bfloat16)
+            for part in range(2):
+                first = part * param_local
+                for chunk in range(chunks):
+                    row = first + chunk * LANES
+                    grouped[chunk, part, f] = sums[row : row + LANES]
+                grouped_tail[f % half_freqs, part, ending] = sums[
+                    first + aligned : first + param_local
+                ]
 
     def group_products(owners, chunk):
         tiles = freq_count if chunk < chunks else half_freqs
@@ -285,27 +291,68 @@
                 )
                 pl.when(target != me_p)(copy.start)
 
-    for owners, product in (([0], near), (list(range(1, qoi_count)), far)):
+    def add_products(owners, product, chunk):
         count = len(owners) * sample_local
+        for f in range(freq_count):
+            for k, value in enumerate(multiply(owners, f, chunk)):
+                for j in range(halves):
+                    here = value[:, j * LANES : (j + 1) * LANES]
+                    if chunk:
+                        here = here + product[j, rows_of(k, f, count), :]
+                    product[j, rows_of(k, f, count), :] = here
+
+    def await_known():
+        pl.semaphore_wait(known, len(contacts))
+
+    def wait_chunk(chunk):
+        rows = freq_count if chunk < chunks else half_freqs
+        wait_line(chunk * freq_count, rows, chunk).wait_recv()
+
+    def send_shares(owners, before_chunk, before_sending, after_chunk):
         totals = None
         for chunk in range(chunks + 1):
-            rows = freq_count if chunk < chunks else half_freqs
-            line_wait = wait_line(chunk * freq_count, rows, chunk)
-            pl.when(me_q != 0 if owners == [0] else me_q == 0)(line_wait.wait_recv)
+            before_chunk(chunk)
             sums = group_products(owners, chunk)
             totals = sums if totals is None else [a + b for a, b in zip(totals, sums)]
             if chunk == chunks:
-                if owners == [0]:
-                    pl.semaphore_wait(known, len(contacts))
+                before_sending()
                 deliver_shares(owners, jnp.concatenate(combine(totals), axis=0))
-            for f in range(freq_count):
-                for k, value in enumerate(multiply(owners, f, chunk)):
-                    for j in range(halves):
-                        here = value[:, j * LANES : (j + 1) * LANES]
-                        if chunk:
-                            here = here + product[j, rows_of(k, f, count), :]
-                        product[j, rows_of(k, f, count), :] = here
+            after_chunk(chunk)
+
+    def nothing(*_):
+        pass
+
+    def receive(owners, product, before_sending):
+        def early(chunk):
+            if chunk < chunks - 1:
+                add_products(owners, product, chunk)
+
+        send_shares(owners, wait_chunk, before_sending, early)
+        for chunk in range(max(chunks - 1, 0), chunks + 1):
+            add_products(owners, product, chunk)
         deliver_blocks(owners, product)
+
+    def serve(owners, product, before_sending, after_blocks):
+        for chunk in range(chunks + 1):
+            add_products(owners, product, chunk)
+        before_sending()
+        deliver_blocks(owners, product)
+        after_blocks()
+        send_shares(owners, nothing, nothing, nothing)
+
+    rest = list(range(1, qoi_count))
+
+    @pl.when(me_q == 0)
+    def _():
+        serve([0], near, await_known, build_grouped)
+        receive(rest, far, nothing)
+
+    @pl.when(me_q != 0)
+    def _():
+        build_grouped()
+        receive([0], near, await_known)
+        serve(rest, far, nothing, nothing)
+
     incoming[me_p] = outgoing[me_p]
     gathered[mine] = shares[me_p]
 

time: 16.3 us -> 16.1 us (0.988)
  no operation moved by 1% of the time
where the time goes in v7:
time: 16.1 us; the launch traced here: 16 us
  Pallas kernels  14.7 us (91%)
  between operations  1.28 us (8%)
    pallas_call x1, Pallas kernels, local(): pl.pallas_call(functools.partial(kernel, param_count, qoi_count), out_sha...  14.1 us
    pallas_call x1, Pallas kernels, local(): pl.pallas_call(writer, out_shape=shapes, in_specs=[vmem, vmem], out_specs...  0.63 us

profile of v7, /device:TPU:0, one launch (start us, length us, event | category | flops | bytes accessed | tf_op | source)
XLA Modules:
  0.0 16.0 jit_solution(11091145855009846511)
XLA Ops:
  1.3 14.1 %shard_map.59 = (f32[1,2,8,256]{3,2,1,0:T(8,128)S(1)}, f32[1,2,8,16]{3,2,1,0:T(8,128)S(1)}) custom-call(s32[1]{0:T(128)S(6)} %copy.7.start_ref, s32[1,256]{1,0:T(1,128)} %bitcast.9, bf16[420,8,320]{2,1,0:T(8,128)(2,1)} %bitcast.8, bf16[8,1280,128]{2,1,0:T(8,128)(2,1)} %bitcast.7), custom_call_target="tpu_custom_call" | custom-call | tf_op jit(solution)/shard_map/pallas_call | solution.py:420
  15.3 0.6 %shard_map.60 = (f32[1,2,8,256]{3,2,1,0:T(8,128)}, f32[1,2,8,16]{3,2,1,0:T(8,128)}) custom-call(f32[1,2,8,256]{3,2,1,0:T(8,128)S(1)} %get-tuple-element.4.spectrum_ref, f32[1,2,8,16]{3,2,1,0:T(8,128)S(1)} %get-tuple-element.5.response_ref), custom_call_target="tpu_custom_call" | custom-call | tf_op jit(solution)/shard_map/pallas_call | solution.py:467

commit v8 on v7

--- a/solution.py
+++ b/solution.py
@@ -10,9 +10,15 @@
 
 GROUPS = 16
 LANES = 128
-LOADS = 2
+LOADS = 1
 MESH = pl.DeviceIdType.MESH
 NT_DIMS = (((1,), (1,)), ((), ()))
+
+
+def pairwise(terms):
+    while len(terms) > 1:
+        terms = [sum(terms[i + 1 : i + 2], terms[i]) for i in range(0, len(terms), 2)]
+    return terms[0]
 
 
 def build_table(start, freq_count, steps_count, count, repeat, table):
@@ -72,8 +78,6 @@
                     (base + lax.rem(me_p + turn, inner), lax.rem(me_q + other, qoi_count))
                 )
     barrier = pltpu.get_barrier_semaphore()
-    group_copy = pltpu.make_async_copy(group_hbm, group_ref, group_sem)
-    group_copy.start()
     lanes = [pl.ds(0, aligned), pl.ds(aligned, tail)]
     sample_copies = [
         pltpu.make_async_copy(samples_hbm.at[:, :, lane], samples.at[:, :, lane], samples_sem.at[part])
@@ -81,6 +85,8 @@
     ]
     for copy in sample_copies:
         copy.start()
+    group_copy = pltpu.make_async_copy(group_hbm, group_ref, group_sem)
+    group_copy.start()
     for contact in contacts:
         pl.semaphore_signal(barrier, inc=1, device_id=contact, device_id_type=MESH)
     per_load = freq_count // LOADS
@@ -368,21 +374,17 @@
         device_id=aside, device_id_type=MESH,
     )
     out_wait.wait_recv()
-    total = incoming[0].astype(jnp.float32)
-    for p in range(1, param_count):
-        total = total + incoming[p].astype(jnp.float32)
+    total = pairwise([incoming[p].astype(jnp.float32) for p in range(param_count)])
     out_ref[...] = total.reshape(out_ref.shape)
+    wait_line(0, chunks * freq_count + half_freqs, 0).wait_send()
+    out_wait.wait_send()
+    share_wait.wait_send()
     share_wait.wait_recv()
-    final = gathered[0]
-    for p in range(1, param_count * qoi_count):
-        final = final + gathered[p]
+    final = pairwise([gathered[p] for p in range(param_count * qoi_count)])
     for k in range(2):
         rows = jnp.broadcast_to(final[k : k + 1], (freq_count, LANES))
         turned = pltpu.roll(rows, 0, 1, stride=GROUPS, stride_axis=0)
         seg_ref[0, k] = turned[:, :GROUPS]
-    wait_line(0, chunks * freq_count + half_freqs, 0).wait_send()
-    out_wait.wait_send()
-    share_wait.wait_send()
 
 
 def writer(spectrum_ref, response_ref, spectrum_hbm, response_hbm, sems):

time: 16.1 us -> 16.1 us (level)
  no operation moved by 1% of the time
where the time goes in v8:
time: 16.1 us; the launch traced here: 15.9 us
  Pallas kernels  14.7 us (91%)
  between operations  1.28 us (8%)
    pallas_call x1, Pallas kernels, local(): pl.pallas_call(functools.partial(kernel, param_count, qoi_count), out_sha...  14 us
    pallas_call x1, Pallas kernels, local(): pl.pallas_call(writer, out_shape=shapes, in_specs=[vmem, vmem], out_specs...  0.63 us

profile of v8, /device:TPU:0, one launch (start us, length us, event | category | flops | bytes accessed | tf_op | source)
XLA Modules:
  0.0 15.9 jit_solution(12241899730791087845)
XLA Ops:
  1.3 14.0 %shard_map.59 = (f32[1,2,8,256]{3,2,1,0:T(8,128)S(1)}, f32[1,2,8,16]{3,2,1,0:T(8,128)S(1)}) custom-call(s32[1]{0:T(128)S(6)} %copy.7.start_ref, s32[1,256]{1,0:T(1,128)} %bitcast.9, bf16[420,8,320]{2,1,0:T(8,128)(2,1)} %bitcast.8, bf16[8,1280,128]{2,1,0:T(8,128)(2,1)} %bitcast.7), custom_call_target="tpu_custom_call" | custom-call | tf_op jit(solution)/shard_map/pallas_call | solution.py:422
  15.3 0.6 %shard_map.60 = (f32[1,2,8,256]{3,2,1,0:T(8,128)}, f32[1,2,8,16]{3,2,1,0:T(8,128)}) custom-call(f32[1,2,8,256]{3,2,1,0:T(8,128)S(1)} %get-tuple-element.4.spectrum_ref, f32[1,2,8,16]{3,2,1,0:T(8,128)S(1)} %get-tuple-element.5.response_ref), custom_call_target="tpu_custom_call" | custom-call | tf_op jit(solution)/shard_map/pallas_call | solution.py:469

commit v9 on v8

--- a/solution.py
+++ b/solution.py
@@ -317,11 +317,12 @@
     def send_shares(owners, before_chunk, before_sending, after_chunk):
         totals = None
         for chunk in range(chunks + 1):
+            if chunk == chunks:
+                before_sending()
             before_chunk(chunk)
             sums = group_products(owners, chunk)
             totals = sums if totals is None else [a + b for a, b in zip(totals, sums)]
             if chunk == chunks:
-                before_sending()
                 deliver_shares(owners, jnp.concatenate(combine(totals), axis=0))
             after_chunk(chunk)
 

time: 16.1 us -> 16.1 us (level)
  no operation moved by 1% of the time
where the time goes in v9:
time: 16.1 us; the launch traced here: 15.9 us
  Pallas kernels  14.7 us (91%)
  between operations  1.28 us (8%)
    pallas_call x1, Pallas kernels, local(): pl.pallas_call(functools.partial(kernel, param_count, qoi_count), out_sha...  14 us
    pallas_call x1, Pallas kernels, local(): pl.pallas_call(writer, out_shape=shapes, in_specs=[vmem, vmem], out_specs...  0.63 us

profile of v9, /device:TPU:0, one launch (start us, length us, event | category | flops | bytes accessed | tf_op | source)
XLA Modules:
  0.0 15.9 jit_solution(7489922898322932556)
XLA Ops:
  1.3 14.0 %shard_map.59 = (f32[1,2,8,256]{3,2,1,0:T(8,128)S(1)}, f32[1,2,8,16]{3,2,1,0:T(8,128)S(1)}) custom-call(s32[1]{0:T(128)S(6)} %copy.7.start_ref, s32[1,256]{1,0:T(1,128)} %bitcast.9, bf16[420,8,320]{2,1,0:T(8,128)(2,1)} %bitcast.8, bf16[8,1280,128]{2,1,0:T(8,128)(2,1)} %bitcast.7), custom_call_target="tpu_custom_call" | custom-call | tf_op jit(solution)/shard_map/pallas_call | solution.py:423
  15.3 0.6 %shard_map.60 = (f32[1,2,8,256]{3,2,1,0:T(8,128)}, f32[1,2,8,16]{3,2,1,0:T(8,128)}) custom-call(f32[1,2,8,256]{3,2,1,0:T(8,128)S(1)} %get-tuple-element.4.spectrum_ref, f32[1,2,8,16]{3,2,1,0:T(8,128)S(1)} %get-tuple-element.5.response_ref), custom_call_target="tpu_custom_call" | custom-call | tf_op jit(solution)/shard_map/pallas_call | solution.py:470
